TPU v7x, 32 devices: a whole 2x2x4 slice. The times are simulated.
32 devices in a mesh: band: 8 (over z, x), dir: 4 (over y, core).
Axes of the slice: x: 2, y: 2, z: 4, core: 2. Of those that a mesh axis runs over, the one named last changes fastest.
Arguments:
- visibilities: bfloat16 [16, 32, 2, 256, 256], P('band', 'dir'), as said below
- sky_model: bfloat16 [16, 32, 2, 256, 256], P('band', 'dir')
- rfi_flags: int32 [16, 8, 8], P('band'), may hold values from 0 to 1, as said below
- destination: int32 [16], P('band'), may hold values from 0 to 15, as said below
Outputs:
- delivered: float32 [16, 32, 2, 256], P('band', 'dir')
- coefficients: float32 [9, 32, 2, 256], P(None, 'dir')
- norm_values: float32 [2, 2], replicated
Inputs may be any that keep to these rules, and one draw needn't show every extreme that they name: `rfi_flags`: 1 marks a flagged baseline block; the share of flagged blocks tends to fall with the subband index. destination holds every row of 0 to 15 once. With the rows split into 8 aligned blocks of 2 rows, one row of block i goes to a row of block i + 1 and the other to a row of block i + 4, modulo 16 // 2. `visibilities`: visibilities follow the model under unknown station gains, with noise.
All inputs are finite; a program needn't handle non-finite values.
Results may differ from a plain program's by a relative error of at most 0.0003.
Values sent between devices are 32-bit elements; how exact they have to be, the bound alone decides.
No kernel may reach another device: no remote copies, remote signals or barrier semaphores. Data moves between devices by JAX's collectives and lax.ppermute only.
A program may use at most 128 MiB of HBM per device.

v0:
```python
import jax
import jax.numpy as jnp
from jax import lax
from jax.sharding import PartitionSpec as P

BLOCK = 32
DEGREE = 8
SWEEPS = 4
ITERS = 2


highest = lax.Precision.HIGHEST
penalty_share = 0.4


def from_behind(block, axis, distance):
    devices = range(lax.axis_size(axis))
    route = [((i - distance) % len(devices), i) for i in devices]
    return lax.ppermute(block, axis, route)


def block_weights(rfi_flags):
    blocks = rfi_flags.shape[-1]
    kept_blocks = (1 - rfi_flags).astype(jnp.float32)
    leading = kept_blocks.shape[:-2]
    spread = jnp.broadcast_to(
        kept_blocks[..., :, None, :, None], leading + (blocks, BLOCK, blocks, BLOCK)
    )
    stations = blocks * BLOCK
    spread = spread.reshape(leading + (stations, stations))
    return spread * (1.0 - jnp.eye(stations, dtype=jnp.float32))


def operators(visibilities, sky_model, rfi_flags):
    baseline = block_weights(rfi_flags)[..., None, :, :]
    data_re = visibilities[..., 0, :, :].astype(jnp.float32)
    data_im = visibilities[..., 1, :, :].astype(jnp.float32)
    model_re = sky_model[..., 0, :, :].astype(jnp.float32)
    model_im = sky_model[..., 1, :, :].astype(jnp.float32)
    oper_re = baseline * (model_re * data_re + model_im * data_im)
    oper_im = baseline * (model_re * data_im - model_im * data_re)
    square = baseline * (model_re * model_re + model_im * model_im)
    return (jnp.stack([oper_re, oper_im], axis=-3), square)


def chebyshev(band_rows, band_total):
    abscissa = (2.0 * band_rows + 1.0) / band_total - 1.0
    cheb_terms = [jnp.ones_like(abscissa), abscissa]
    for degree in range(2, DEGREE + 1):
        cheb_terms.append(2.0 * abscissa * cheb_terms[-1] - cheb_terms[-2])
    return jnp.stack(cheb_terms[: DEGREE + 1], axis=0)


def stefcal(operator, square, gain_now, target, penalty):
    pen_term = penalty[..., None, None, None]
    for sweep_index in range(SWEEPS):
        products = jnp.einsum("...kapq,...kbq->...kabp", operator, gain_now, precision=highest)
        real_part = products[..., 0, 0, :] - products[..., 1, 1, :]
        imag_part = products[..., 0, 1, :] + products[..., 1, 0, :]
        numerator = jnp.stack([real_part, imag_part], axis=-2)
        magnitude = jnp.sum(gain_now * gain_now, axis=-2)
        denominator = jnp.einsum("...kpq,...kq->...kp", square, magnitude, precision=highest)
        updated = (numerator + pen_term * target) / (denominator[..., None, :] + pen_term)
        gain_now = 0.5 * (updated + gain_now) if sweep_index % 2 == 1 else updated
    return gain_now


def per_device(visibilities, sky_model, rfi_flags, destination):
    local_bands = visibilities.shape[0]
    local_dirs = visibilities.shape[1]
    stations = visibilities.shape[-1]
    blocks = rfi_flags.shape[-1]
    band_index = lax.axis_index("band")
    band_count = lax.axis_size("band")
    band_total = local_bands * band_count
    operator, square = operators(visibilities, sky_model, rfi_flags)
    weights = (1.0 + jnp.sum(1 - rfi_flags, axis=(1, 2)).astype(jnp.float32)) / (
        1.0 + blocks * blocks
    )
    penalty = penalty_share * stations * weights
    band_rows = (band_index * local_bands + jnp.arange(local_bands)).astype(jnp.float32)
    cheb_basis = chebyshev(band_rows, band_total)
    weighted = cheb_basis * weights[None, :]
    gram_part = jnp.dot(weighted, cheb_basis.T, precision=highest)
    ones_part = jnp.ones((local_bands, local_dirs, stations), jnp.float32)
    unit_gains = jnp.stack([ones_part, jnp.zeros_like(ones_part)], axis=2)
    gain_now = unit_gains
    consensus = unit_gains
    dual_var = jnp.zeros_like(unit_gains)
    row_weight = weights[:, None, None, None]
    norm_rows = []
    gram_matrix = gram_part
    coefficients = None
    for iteration in range(ITERS):
        gain_now = stefcal(operator, square, gain_now, consensus - dual_var, penalty)
        projection = jnp.einsum("cs,skap->ckap", weighted, gain_now + dual_var, precision=highest)
        projection, gram_matrix = lax.psum((projection, gram_part), "band")
        factor = jnp.linalg.cholesky(gram_matrix)
        flat_proj = projection.reshape(projection.shape[0], -1)
        coefficients = jax.scipy.linalg.cho_solve((factor, True), flat_proj).reshape(
            projection.shape
        )
        fresh_gains = jnp.einsum("cs,ckap->skap", cheb_basis, coefficients, precision=highest)
        dual_var = dual_var + gain_now - fresh_gains
        local_terms = jnp.stack(
            [
                jnp.sum(row_weight * (gain_now - fresh_gains) ** 2),
                jnp.sum(row_weight * (fresh_gains - consensus) ** 2),
            ]
        )
        consensus = fresh_gains
        norm_rows.append(lax.psum(local_terms, ("band", "dir")))
    totals = jnp.stack(norm_rows)
    normalizer = local_dirs * lax.axis_size("dir") * 2.0 * stations * gram_matrix[0, 0]
    norm_values = jnp.sqrt(totals / normalizer)
    flat_gains = gain_now.reshape(local_bands, -1)
    dest_float = destination.astype(jnp.float32)
    near_gains, near_dest = from_behind((flat_gains, dest_float), "band", 1)
    far_gains, far_dest = from_behind((flat_gains, dest_float), "band", band_count // 2)
    all_gains = jnp.concatenate([flat_gains, near_gains, far_gains], axis=0)
    all_dest = jnp.concatenate([dest_float, near_dest, far_dest], axis=0)
    selector = (all_dest[None, :] == band_rows[:, None]).astype(jnp.float32)
    delivered = jnp.dot(selector, all_gains, precision=highest)
    return (delivered.reshape(gain_now.shape), coefficients, norm_values)


def solution(mesh):
    return jax.shard_map(
        per_device,
        mesh=mesh,
        in_specs=(
            P("band", "dir", None, None, None),
            P("band", "dir", None, None, None),
            P("band", None, None),
            P("band"),
        ),
        out_specs=(P("band", "dir", None, None), P(None, "dir", None, None), P()),
        check_vma=False,
    )
```

profile of v0, /device:TPU:0, one launch (start us, length us, event | category | flops | bytes accessed | tf_op | source)
XLA Modules:
  0.0 308.3 jit_solution(2496416499271665687)
XLA Ops:
  7.9 4.1 %collective-permute-start.1 = (f32[2]{0:T(128)S(1)}, f32[2]{0:T(128)S(1)}, u32[]{:S(2)}, u32[]{:S(2)}) collective-permute-start(f32[2]{0:T(128)S(1)} %convert_element_type.93), channel_id=1, source_target_pairs={{16,0},{20,4},{24,8},{28,12},{0,16},{4,20},{8,24},{12,28},{17,1},{... | collective-permute-start | bytes 32 | tf_op jit(solution)/shard_map/ppermute | solution.py:19
  15.3 6.7 %fusion.91 = f32[2,8,1,256]{3,2,1,0:T(1,128)S(1)} fusion(f32[2,256,256]{2,1,0:T(8,128)S(1)} %broadcast_multiply_fusion, bf16[2,8,2,256,256]{4,3,2,1,0:T(8,128)(2,1)} %param.8), kind=kOutput, calls=%fused_computation.155 | convolution fusion | flops 18874368 | bytes 4734976 | tf_op jit(solution)/shard_map/...kpq,...kq->...kp/dot_general | solution.py:62
  22.0 1.9 fusion.1
  24.0 6.9 %fusion.107 = f32[2,8,2,2,256]{4,2,3,1,0:T(2,128)S(1)} fusion(f32[2,8,2,256,1]{3,2,4,1,0:T(2,128)S(1)} %copy-done.10, f32[2,8,1,256,256]{4,3,2,1,0:T(8,128)S(1)} %get-tuple-element.29, f32[2,8,1,256,256]{4,3,2,1,0:T(8,128)S(1)} %get-tuple-element.28), kind=kOutput, calls=%fused_computation.194 | convolution fusion | flops 52428800 | bytes 8486912 | tf_op jit(solution)/shard_map/...kapq,...kbq->...kabp/dot_general | solution.py:57
  31.1 4.4 %fusion.79 = f32[2,8,1,256]{3,2,1,0:T(1,128)S(1)} fusion(f32[2,8,256,1]{2,1,0,3:T(8,128)S(1)} %bitcast.186, f32[2,256,256]{2,1,0:T(8,128)S(1)} %broadcast_multiply_fusion, bf16[2,8,2,256,256]{4,3,2,1,0:T(8,128)(2,1)S(1)} %copy-done.6), kind=kOutput, calls=%fused_computation.142 | convolution fusion | flops 18874368 | bytes 4751360 | tf_op jit(solution)/shard_map/...kpq,...kq->...kp/dot_general | solution.py:62
  35.6 7.1 %fusion.45 = f32[2,8,2,2,256]{4,2,3,1,0:T(2,128)S(1)} fusion(f32[2,8,2,256,1]{3,1,2,0,4:T(8,128)S(1)} %bitcast.170, f32[2,8,1,256,256]{4,3,2,1,0:T(8,128)S(1)} %get-tuple-element.29, f32[2,8,1,256,256]{4,3,2,1,0:T(8,128)S(1)} %get-tuple-element.28), kind=kOutput, calls=%fused_computation.71 | convolution fusion | flops 52428800 | bytes 8486912 | tf_op jit(solution)/shard_map/...kapq,...kbq->...kabp/dot_general | solution.py:57
  42.8 4.4 %fusion.77 = f32[2,8,1,256]{3,2,1,0:T(1,128)S(1)} fusion(f32[2,8,256,1]{2,1,0,3:T(8,128)S(1)} %bitcast.182, f32[2,256,256]{2,1,0:T(8,128)S(1)} %broadcast_multiply_fusion, bf16[2,8,2,256,256]{4,3,2,1,0:T(8,128)(2,1)S(1)} %copy-done.6), kind=kOutput, calls=%fused_computation.140 | convolution fusion | flops 18874368 | bytes 4751360 | tf_op jit(solution)/shard_map/...kpq,...kq->...kp/dot_general | solution.py:62
  47.2 7.3 %fusion.43 = f32[2,8,2,2,256]{4,2,3,1,0:T(2,128)S(1)} fusion(f32[2,8,2,256,1]{3,1,2,0,4:T(8,128)S(1)} %bitcast.179, f32[2,8,1,256,256]{4,3,2,1,0:T(8,128)S(1)} %get-tuple-element.29, f32[2,8,1,256,256]{4,3,2,1,0:T(8,128)S(1)} %get-tuple-element.28), kind=kOutput, calls=%fused_computation.69 | convolution fusion | flops 52428800 | bytes 8486912 | tf_op jit(solution)/shard_map/...kapq,...kbq->...kabp/dot_general | solution.py:57
  54.7 4.4 %fusion.75 = f32[2,8,1,256]{3,2,1,0:T(1,128)S(1)} fusion(f32[2,8,256,1]{2,1,0,3:T(8,128)S(1)} %bitcast.187, f32[2,256,256]{2,1,0:T(8,128)S(1)} %broadcast_multiply_fusion, bf16[2,8,2,256,256]{4,3,2,1,0:T(8,128)(2,1)S(1)} %copy-done.6), kind=kOutput, calls=%fused_computation.138 | convolution fusion | flops 18874368 | bytes 4751360 | tf_op jit(solution)/shard_map/...kpq,...kq->...kp/dot_general | solution.py:62
  59.1 6.9 %fusion.41 = f32[2,8,2,2,256]{4,2,3,1,0:T(2,128)S(1)} fusion(f32[2,8,2,256,1]{3,1,2,0,4:T(8,128)S(1)} %bitcast.168, f32[2,8,1,256,256]{4,3,2,1,0:T(8,128)S(1)} %get-tuple-element.29, f32[2,8,1,256,256]{4,3,2,1,0:T(8,128)S(1)} %get-tuple-element.28), kind=kOutput, calls=%fused_computation.67 | convolution fusion | flops 52428800 | bytes 8486912 | tf_op jit(solution)/shard_map/...kapq,...kbq->...kabp/dot_general | solution.py:57
  68.0 20.9 %psum.38 = f32[9,9]{0,1:T(8,128)S(1)} all-reduce(f32[9,9]{0,1:T(8,128)S(1)} %fusion.95), channel_id=1, replica_groups=mesh['band'=8,'dir'=4] {'band'}, use_global_device_ids=true, to_apply=%region_4.0 | all-reduce | flops 81 | bytes 648 | tf_op jit(solution)/shard_map/psum | solution.py:97
  91.5 6.6 %fusion.73 = f32[2,8,1,256]{3,2,1,0:T(1,128)S(1)} fusion(f32[2,8,256,1]{2,1,0,3:T(8,128)S(1)} %bitcast.181, f32[2,256,256]{2,1,0:T(8,128)S(1)} %broadcast_multiply_fusion, bf16[2,8,2,256,256]{4,3,2,1,0:T(8,128)(2,1)} %param.8), kind=kOutput, calls=%fused_computation.136 | convolution fusion | flops 18874368 | bytes 4751360 | tf_op jit(solution)/shard_map/...kpq,...kq->...kp/dot_general | solution.py:62
  98.2 9.1 %fusion.39 = f32[2,8,2,2,256]{4,2,3,1,0:T(2,128)S(1)} fusion(f32[2,8,2,256,1]{3,1,2,0,4:T(8,128)S(1)} %bitcast.166, f32[2,8,1,256,256]{4,3,2,1,0:T(8,128)} %copy-done.3, f32[2,8,1,256,256]{4,3,2,1,0:T(8,128)S(1)} %copy-done.1), kind=kOutput, calls=%fused_computation.65 | convolution fusion | flops 52428800 | bytes 8486912 | tf_op jit(solution)/shard_map/...kapq,...kbq->...kabp/dot_general | solution.py:57
  109.3 29.9 %all-reduce.4.cloned.1.call-done = f32[9,4096]{1,0:T(8,128)} async-done(((f32[9,4096]{1,0:T(8,128)}), f32[9,4096]{1,0:T(8,128)}) %all-reduce.4.cloned.1.call-update) | async-done | bytes 147472 | tf_op jit(solution)/shard_map/psum | solution.py:97
  141.5 7.0 %fusion.71 = f32[2,8,1,256]{3,2,1,0:T(1,128)S(1)} fusion(f32[2,8,256,1]{2,1,0,3:T(8,128)S(1)} %bitcast.183, f32[2,256,256]{2,1,0:T(8,128)S(1)} %broadcast_multiply_fusion, bf16[2,8,2,256,256]{4,3,2,1,0:T(8,128)(2,1)} %param.8), kind=kOutput, calls=%fused_computation.134 | convolution fusion | flops 18874368 | bytes 4751360 | tf_op jit(solution)/shard_map/...kpq,...kq->...kp/dot_general | solution.py:62
  148.6 6.9 %fusion.37 = f32[2,8,2,2,256]{4,2,3,1,0:T(2,128)S(1)} fusion(f32[2,8,2,256,1]{3,1,2,0,4:T(8,128)S(1)} %bitcast.169, f32[2,8,1,256,256]{4,3,2,1,0:T(8,128)S(1)} %copy-done.4, f32[2,8,1,256,256]{4,3,2,1,0:T(8,128)S(1)} %copy-done.2), kind=kOutput, calls=%fused_computation.63 | convolution fusion | flops 52428800 | bytes 8486912 | tf_op jit(solution)/shard_map/...kapq,...kbq->...kabp/dot_general | solution.py:57
  155.6 4.4 %fusion.69 = f32[2,8,1,256]{3,2,1,0:T(1,128)S(1)} fusion(f32[2,8,256,1]{2,1,0,3:T(8,128)S(1)} %bitcast.184, f32[2,256,256]{2,1,0:T(8,128)S(1)} %broadcast_multiply_fusion, bf16[2,8,2,256,256]{4,3,2,1,0:T(8,128)(2,1)S(1)} %copy-done.7), kind=kOutput, calls=%fused_computation.132 | convolution fusion | flops 18874368 | bytes 4751360 | tf_op jit(solution)/shard_map/...kpq,...kq->...kp/dot_general | solution.py:62
  160.0 7.3 %fusion.35 = f32[2,8,2,2,256]{4,2,3,1,0:T(2,128)S(1)} fusion(f32[2,8,2,256,1]{3,1,2,0,4:T(8,128)S(1)} %bitcast.180, f32[2,8,1,256,256]{4,3,2,1,0:T(8,128)S(1)} %copy-done.4, f32[2,8,1,256,256]{4,3,2,1,0:T(8,128)S(1)} %copy-done.2), kind=kOutput, calls=%fused_computation.61 | convolution fusion | flops 52428800 | bytes 8486912 | tf_op jit(solution)/shard_map/...kapq,...kbq->...kabp/dot_general | solution.py:57
  167.4 4.4 %fusion.67 = f32[2,8,1,256]{3,2,1,0:T(1,128)S(1)} fusion(f32[2,8,256,1]{2,1,0,3:T(8,128)S(1)} %bitcast.185, f32[2,256,256]{2,1,0:T(8,128)S(1)} %broadcast_multiply_fusion, bf16[2,8,2,256,256]{4,3,2,1,0:T(8,128)(2,1)S(1)} %copy-done.7), kind=kOutput, calls=%fused_computation.130 | convolution fusion | flops 18874368 | bytes 4751360 | tf_op jit(solution)/shard_map/...kpq,...kq->...kp/dot_general | solution.py:62
  171.9 7.1 %fusion.33 = f32[2,8,2,2,256]{4,2,3,1,0:T(2,128)S(1)} fusion(f32[2,8,2,256,1]{3,1,2,0,4:T(8,128)S(1)} %bitcast.167, f32[2,8,1,256,256]{4,3,2,1,0:T(8,128)S(1)} %copy-done.4, f32[2,8,1,256,256]{4,3,2,1,0:T(8,128)S(1)} %copy-done.2), kind=kOutput, calls=%fused_computation.59 | convolution fusion | flops 52428800 | bytes 8486912 | tf_op jit(solution)/shard_map/...kapq,...kbq->...kabp/dot_general | solution.py:57
  179.1 1.7 collective-permute-start.3
  184.0 3.5 %collective-permute-done.2 = f32[2,4096]{1,0:T(2,128)S(1)} collective-permute-done((f32[2,4096]{1,0:T(2,128)S(1)}, f32[2,4096]{1,0:T(2,128)S(1)}, u32[]{:S(2)}, u32[]{:S(2)}) %collective-permute-start.2) | collective-permute-done | bytes 32800 | tf_op jit(solution)/shard_map/ppermute | solution.py:19
  187.7 67.2 %all-reduce.6.cloned.1.call-done = f32[9,4096]{1,0:T(8,128)} async-done(((f32[9,4096]{1,0:T(8,128)}), f32[9,4096]{1,0:T(8,128)}) %all-reduce.6.cloned.1.call-update) | async-done | bytes 147472 | tf_op jit(solution)/shard_map/psum | solution.py:97
  261.2 39.5 %all-reduce = (f32[1,2]{1,0:T(1,128)S(1)}, f32[1,2]{1,0:T(1,128)S(1)}) all-reduce(f32[1,2]{1,0:T(1,128)S(1)} %maximum_bitcast_fusion.1, f32[1,2]{1,0:T(1,128)S(1)} %maximum_bitcast_fusion), channel_id=1, replica_groups=mesh['band'=8,'dir'=4] {'band','dir'}, use_global_device_ids=true, to_apply=%region_18.0 | all-reduce | flops 4 | bytes 32 | tf_op jit(solution)/shard_map/psum | solution.py:112
  (111 shorter events, 23.5 us)
Async XLA Ops:
  7.2 132.0 %all-reduce.4.cloned.1.call-start = ((), (), s32[]{:S(2)}) async-start(), calls=%async_computation | async-start | bytes 524288 | tf_op jit(solution)/shard_map/psum | solution.py:97
  7.9 101.4 %collective-permute-start.1 = (f32[2]{0:T(128)S(1)}, f32[2]{0:T(128)S(1)}, u32[]{:S(2)}, u32[]{:S(2)}) collective-permute-start(f32[2]{0:T(128)S(1)} %convert_element_type.93), channel_id=1, source_target_pairs={{16,0},{20,4},{24,8},{28,12},{0,16},{4,20},{8,24},{12,28},{17,1},{... | collective-permute-start | bytes 32 | tf_op jit(solution)/shard_map/ppermute | solution.py:19
  11.9 97.3 %collective-permute-start = (f32[2]{0:T(128)S(1)}, f32[2]{0:T(128)S(1)}, u32[]{:S(2)}, u32[]{:S(2)}) collective-permute-start(f32[2]{0:T(128)S(1)} %convert_element_type.93), channel_id=1, source_target_pairs={{28,0},{0,4},{4,8},{8,12},{12,16},{16,20},{20,24},{24,28},{29,1},{... | collective-permute-start | bytes 32 | tf_op jit(solution)/shard_map/ppermute | solution.py:19
  15.2 6.8 %copy-start.6 = (bf16[2,8,2,256,256]{4,3,2,1,0:T(8,128)(2,1)S(1)}, bf16[2,8,2,256,256]{4,3,2,1,0:T(8,128)(2,1)}, u32[]{:S(2)}) copy-start(bf16[2,8,2,256,256]{4,3,2,1,0:T(8,128)(2,1)} %param.8) | copy-start | bytes 12582916
  15.3 6.8 %copy-start.5 = (bf16[2,8,2,256,256]{4,3,2,1,0:T(8,128)(2,1)S(1)}, bf16[2,8,2,256,256]{4,3,2,1,0:T(8,128)(2,1)}, u32[]{:S(2)}) copy-start(bf16[2,8,2,256,256]{4,3,2,1,0:T(8,128)(2,1)} %param.7) | copy-start | bytes 12582916
  22.0 2.0 copy-start.10
  24.0 35.2 %copy-start = (f32[2,8,1,256,256]{4,3,2,1,0:T(8,128)}, f32[2,8,1,256,256]{4,3,2,1,0:T(8,128)S(1)}, u32[]{:S(2)}) copy-start(f32[2,8,1,256,256]{4,3,2,1,0:T(8,128)S(1)} %get-tuple-element.28) | copy-start | bytes 12582916
  24.0 35.1 %copy-start.3 = (f32[2,8,1,256,256]{4,3,2,1,0:T(8,128)}, f32[2,8,1,256,256]{4,3,2,1,0:T(8,128)S(1)}, u32[]{:S(2)}) copy-start(f32[2,8,1,256,256]{4,3,2,1,0:T(8,128)S(1)} %get-tuple-element.29) | copy-start | bytes 12582916
  24.0 7.0 %copy-start.9 = (f32[2,8,2,256]{3,1,2,0:T(8,128)S(1)}, f32[2,8,2,256]{3,1,2,0:T(8,128)}, u32[]{:S(2)}) copy-start(f32[2,8,2,256]{3,1,2,0:T(8,128)} %constant.65.clone.1) | copy-start | bytes 98308
  67.8 187.1 %all-reduce.6.cloned.1.call-start = ((), (), s32[]{:S(2)}) async-start(), calls=%async_computation.1 | async-start | bytes 524288 | tf_op jit(solution)/shard_map/psum | solution.py:97
  89.8 8.4 %copy-start.1 = (f32[2,8,1,256,256]{4,3,2,1,0:T(8,128)S(1)}, f32[2,8,1,256,256]{4,3,2,1,0:T(8,128)}, u32[]{:S(2)}) copy-start(f32[2,8,1,256,256]{4,3,2,1,0:T(8,128)} %copy-done) | copy-start | bytes 12582916
  141.0 7.5 %copy-start.2 = (f32[2,8,1,256,256]{4,3,2,1,0:T(8,128)S(1)}, f32[2,8,1,256,256]{4,3,2,1,0:T(8,128)}, u32[]{:S(2)}) copy-start(f32[2,8,1,256,256]{4,3,2,1,0:T(8,128)} %copy-done) | copy-start | bytes 12582916
  141.1 7.5 %copy-start.4 = (f32[2,8,1,256,256]{4,3,2,1,0:T(8,128)S(1)}, f32[2,8,1,256,256]{4,3,2,1,0:T(8,128)}, u32[]{:S(2)}) copy-start(f32[2,8,1,256,256]{4,3,2,1,0:T(8,128)} %copy-done.3) | copy-start | bytes 12582916
  148.6 7.0 %copy-start.7 = (bf16[2,8,2,256,256]{4,3,2,1,0:T(8,128)(2,1)S(1)}, bf16[2,8,2,256,256]{4,3,2,1,0:T(8,128)(2,1)}, u32[]{:S(2)}) copy-start(bf16[2,8,2,256,256]{4,3,2,1,0:T(8,128)(2,1)} %param.8) | copy-start | bytes 12582916
  171.9 85.2 %copy-start.11 = (f32[2,8,2,256]{3,1,2,0:T(8,128)S(1)}, f32[2,8,2,256]{3,1,2,0:T(8,128)}, u32[]{:S(2)}) copy-start(f32[2,8,2,256]{3,1,2,0:T(8,128)} %constant.76.clone.1) | copy-start | bytes 98308
  179.1 4.9 %collective-permute-start.3 = (f32[2,4096]{1,0:T(2,128)S(1)}, f32[2,4096]{1,0:T(2,128)S(1)}, u32[]{:S(2)}, u32[]{:S(2)}) collective-permute-start(f32[2,4096]{1,0:T(2,128)S(1)} %reshape.458), channel_id=1, source_target_pairs={{16,0},{20,4},{24,8},{28,12},{0,16},{4,20},{8,24},{12,28},{17,1},{... | collective-permute-start | bytes 98312 | tf_op jit(solution)/shard_map/ppermute | solution.py:19
  180.8 6.6 %collective-permute-start.2 = (f32[2,4096]{1,0:T(2,128)S(1)}, f32[2,4096]{1,0:T(2,128)S(1)}, u32[]{:S(2)}, u32[]{:S(2)}) collective-permute-start(f32[2,4096]{1,0:T(2,128)S(1)} %reshape.458), channel_id=1, source_target_pairs={{28,0},{0,4},{4,8},{8,12},{12,16},{16,20},{20,24},{24,28},{29,1},{... | collective-permute-start | bytes 98312 | tf_op jit(solution)/shard_map/ppermute | solution.py:19
  256.7 44.5 %copy-start.8 = (f32[9,8,2,256]{3,2,1,0:T(2,128)}, f32[9,8,2,256]{3,2,1,0:T(2,128)S(1)}, u32[]{:S(2)}) copy-start(f32[9,8,2,256]{3,2,1,0:T(2,128)S(1)} %reshape.461) | copy-start | bytes 442372
Sparse Core Ops, SparseCore 0:
  67.9 71.2 all-reduce.3
  183.9 70.9 all-reduce.5
where the time goes:
time: 313 us; the launch traced here: 308 us
  matrix products  106 us (34%)
  waiting for transfers between devices  101 us (32%)
  blocking collectives  60.4 us (19%)
  between operations  15.4 us (5%)
  other arithmetic  11.9 us (4%)
  starting transfers between devices  8.79 us (3%)
  local copies, waits for them, and re-layouts  4.65 us (1%)
    psum x2, waiting for transfers between devices, per_device(): projection, gram_matrix = lax.psum((projection, gram_part), 'band')  97 us
    dot_general x8, matrix products, stefcal(): jnp.einsum('...kapq,...kbq->...kabp', operator, gain_now, precision=highest)  58.6 us
    dot_general x8, matrix products, stefcal(): jnp.einsum('...kpq,...kq->...kp', square, magnitude, precision=highest)  42.2 us
    psum x1, blocking collectives, per_device(): norm_rows.append(lax.psum(local_terms, ('band', 'dir')))  39.5 us
    psum x1, blocking collectives, per_device(): projection, gram_matrix = lax.psum((projection, gram_part), 'band')  20.9 us
    ppermute x4, starting transfers between devices, from_behind(): return lax.ppermute(block, axis, route)  8.72 us
  transfers between devices with their start and end apart: 6, of which 4 were waited for; matrix products, arithmetic and copies ran while one was open for 25% of the time, Pallas kernels for 0%

commit v1 on v0

v1 whole, which is shorter than its diff:
```python
import functools

import jax
import jax.numpy as jnp
from jax import lax
from jax.experimental import pallas as pl
from jax.experimental.pallas import tpu as pltpu
from jax.sharding import PartitionSpec as P

DEGREE = 8
SWEEPS = 4
ITERS = 2
PENALTY_SHARE = 0.4
LANES = 128
SUBLANES = 8

highest = lax.Precision.HIGHEST
f32 = jnp.float32
bf16 = jnp.bfloat16


def round_up(value, step):
    return -(-value // step) * step


def roll_rows(x, shift):
    return pltpu.roll(x, shift % x.shape[0], 0)


def row_pattern(stations):
    rows = lax.broadcasted_iota(jnp.int32, (SUBLANES, stations), 0)
    even = rows % 2 == 0
    first = rows % 4 < 2
    return even, first


def split_rows(x, even):
    high = x.astype(bf16).astype(f32)
    return jnp.where(even, high, x - high)


def add_pairs(x, even):
    return x + jnp.where(even, roll_rows(x, -1), roll_rows(x, 1))


def sweep(load_oper, gain, target_term, pen, average, even, first):
    stations = gain.shape[1]
    halves = split_rows(gain, even)
    crossed = roll_rows(halves, 2)
    crossed = jnp.where(first, -crossed, crossed)
    square = gain * gain
    magnitude = split_rows(square + roll_rows(square, 2), even)
    halves, crossed, magnitude = [v.astype(bf16) for v in (halves, crossed, magnitude)]
    lhs = jnp.concatenate([halves, halves, crossed, crossed], axis=1)
    numerator = jnp.dot(lhs, load_oper(0, 4 * stations), preferred_element_type=f32)
    lhs = jnp.concatenate([magnitude, magnitude], axis=1)
    denominator = jnp.dot(
        lhs, load_oper(4 * stations, 2 * stations), preferred_element_type=f32
    )
    numerator = add_pairs(numerator, even)
    denominator = add_pairs(denominator, even)
    updated = (numerator + target_term) / (denominator + pen)
    return 0.5 * (updated + gain) if average else updated


def to_rows(real, imag, first):
    return jnp.where(first, real, imag)


def band_weight(flags_ref, f, blocks):
    flagged = jnp.int32(0)
    for i in range(blocks):
        for j in range(blocks):
            flagged = flagged + flags_ref[f, i, j]
    kept = (blocks * blocks - flagged).astype(f32)
    return (1.0 + kept) / (1.0 + blocks * blocks)


def first_kernel(
    flags_ref, dest_ref, vis_ref, sky_ref, oper_ref, gain_ref, mask_ref, turned_ref
):
    step = pl.program_id(0)
    bands, group, _, stations, _ = vis_ref.shape
    blocks = flags_ref.shape[-1]
    block = stations // blocks
    lanes = gain_ref.shape[1] - LANES
    even, first = row_pattern(stations)

    @pl.when(step == 0)
    def _():
        cols = lax.broadcasted_iota(jnp.int32, (block, stations), 1)
        rows = lax.broadcasted_iota(jnp.int32, (block, stations), 0)
        for f in range(bands):
            for i in range(blocks):
                keep = jnp.zeros((block, stations), f32)
                for j in range(blocks):
                    value = (1 - flags_ref[f, i, j]).astype(f32)
                    keep = jnp.where(cols // block == j, value, keep)
                keep = jnp.where(cols == rows + i * block, 0.0, keep)
                mask_ref[f, pl.ds(i * block, block), :] = keep.astype(bf16)
            weight = band_weight(flags_ref, f, blocks)
            lane = lax.broadcasted_iota(jnp.int32, (1, LANES), 1)
            extra = jnp.where(lane == 0, weight, dest_ref[f].astype(f32))
            gain_ref[pl.ds(f, 1), pl.ds(lanes, LANES)] = extra

    chunk = 32
    gains = []
    penalties = []
    for f in range(bands):
        weight = band_weight(flags_ref, f, blocks)
        pen = PENALTY_SHARE * stations * weight
        for k in range(group):
            pair = (step * group + k) * bands + f
            mask = mask_ref[f]
            for a in range(2):
                turned_ref[a] = (sky_ref[f, k, a] * mask).T
                turned_ref[2 + a] = vis_ref[f, k, a].T
            totals = [jnp.zeros((SUBLANES, stations), f32) for _ in range(3)]
            for c in range(stations // chunk):
                part = pl.ds(c * chunk, chunk)
                model_re, model_im, data_re, data_im = [
                    turned_ref[a, part, :].astype(f32) for a in range(4)
                ]
                values = (
                    model_re * data_re + model_im * data_im,
                    model_re * data_im - model_im * data_re,
                    model_re * model_re + model_im * model_im,
                )
                for n, value in enumerate(values):
                    high = value.astype(bf16)
                    low = (value - high.astype(f32)).astype(bf16)
                    start = 2 * n * stations + c * chunk
                    oper_ref[pair, pl.ds(start, chunk), :] = high
                    oper_ref[pair, pl.ds(start + stations, chunk), :] = low
                    for r in range(chunk // SUBLANES):
                        totals[n] = totals[n] + value[r * SUBLANES : (r + 1) * SUBLANES]
            sums = [jnp.sum(t, axis=0, keepdims=True) for t in totals]
            scale = sums[2] + pen
            real = (sums[0] + pen) / scale
            imag = sums[1] / scale
            gains.append(to_rows(real, imag, first))
            penalties.append(pen)
    for index in range(1, SWEEPS):
        number = 0
        for f in range(bands):
            for k in range(group):
                pair = (step * group + k) * bands + f
                pen = penalties[number]

                def load_oper(start, size, pair=pair):
                    return oper_ref[pair, pl.ds(start, size), :]

                target_term = jnp.where(first, pen, 0.0)
                gains[number] = sweep(
                    load_oper, gains[number], target_term, pen, index % 2 == 1, even, first
                )
                number += 1
    number = 0
    for f in range(bands):
        for k in range(group):
            for a in range(2):
                start = pl.multiple_of(((step * group + k) * 2 + a) * stations, stations)
                gain_ref[pl.ds(f, 1), pl.ds(start, stations)] = gains[number][
                    2 * a : 2 * a + 1
                ]
            number += 1


def chebyshev_columns(abscissa, width):
    lane = lax.broadcasted_iota(jnp.int32, (abscissa.shape[0], width), 1)
    terms = [jnp.ones_like(abscissa), abscissa]
    for degree in range(2, DEGREE + 1):
        terms.append(2.0 * abscissa * terms[-1] - terms[-2])
    basis = jnp.zeros((abscissa.shape[0], width), f32)
    for degree in range(DEGREE + 1):
        basis = jnp.where(lane == degree, terms[degree], basis)
    return basis


def fit_matrix(basis, weight):
    rows, width = basis.shape
    terms = round_up(DEGREE + 1, SUBLANES)
    span = round_up(rows, LANES)
    lane = lax.broadcasted_iota(jnp.int32, (rows, span), 1)
    row = lax.broadcasted_iota(jnp.int32, (rows, span), 0)
    identity = jnp.where(lane == row, 1.0, 0.0)
    weighted = basis * weight
    right = jnp.concatenate([basis, identity], axis=1)
    system = lax.dot_general(
        weighted, right, (((0,), (0,)), ((), ())), precision=highest,
        preferred_element_type=f32,
    )[:terms]
    line = lax.broadcasted_iota(jnp.int32, system.shape, 0)
    for j in range(DEGREE + 1):
        pivot = system[j : j + 1] / system[j : j + 1, j : j + 1]
        system = jnp.where(line == j, pivot, system - system[:, j : j + 1] * pivot)
    return system[:, width : width + rows], system[0:1, 0:1]


def second_kernel(
    index_ref, flags_ref, all_ref, oper_ref, gain_ref, fresh_ref, dual_ref, fit_ref
):
    bands = gain_ref.shape[0]
    lanes = gain_ref.shape[1]
    rows = all_ref.shape[0]
    blocks = flags_ref.shape[-1]
    pairs = oper_ref.shape[0]
    stations = oper_ref.shape[2]
    even, first = row_pattern(stations)
    basis = gathered_basis(index_ref[0], bands, rows)
    weight = all_ref[:, pl.ds(lanes, 1)]
    fit, _ = fit_matrix(basis, weight)
    fit_ref[...] = jnp.zeros_like(fit_ref)
    fit_ref[:, pl.ds(0, rows)] = fit
    project = jnp.dot(
        basis[:, : fit.shape[0]], fit, precision=highest, preferred_element_type=f32
    )
    own = all_ref[:, pl.ds(0, lanes)]
    fresh = jnp.dot(project, own, precision=highest, preferred_element_type=f32)
    fresh_ref[...] = fresh
    dual_ref[...] = own - fresh
    group = 4
    for start in range(0, pairs, group):
        gains = []
        targets = []
        penalties = []
        for pair in range(start, start + group):
            k, f = divmod(pair, bands)
            pen = PENALTY_SHARE * stations * band_weight(flags_ref, f, blocks)
            parts = [pl.ds((2 * k + a) * stations, stations) for a in range(2)]
            line = pl.ds(f, 1)
            gains.append(
                to_rows(all_ref[line, parts[0]], all_ref[line, parts[1]], first)
            )
            goal = [fresh_ref[line, p] - dual_ref[line, p] for p in parts]
            targets.append(pen * to_rows(goal[0], goal[1], first))
            penalties.append(pen)
        for index in range(SWEEPS):
            for n in range(group):
                pair = start + n

                def load_oper(begin, size, pair=pair):
                    return oper_ref[pair, pl.ds(begin, size), :]

                gains[n] = sweep(
                    load_oper, gains[n], targets[n], penalties[n], index % 2 == 1, even, first
                )
        for n in range(group):
            k, f = divmod(start + n, bands)
            for a in range(2):
                gain_ref[pl.ds(f, 1), pl.ds((2 * k + a) * stations, stations)] = gains[n][
                    2 * a : 2 * a + 1
                ]


def gathered_basis(index, bands, rows):
    row = lax.broadcasted_iota(jnp.int32, (rows, LANES), 0)
    band_row = ((row // bands) ^ index) * bands + row % bands
    abscissa = (2.0 * band_row.astype(f32) + 1.0) / rows - 1.0
    return chebyshev_columns(abscissa, LANES)


def third_kernel(
    index_ref, last_ref, all_ref, fresh_ref, dual_ref, fit_ref,
    delivered_ref, coefficients_ref, norm_ref,
):
    bands, dirs, _, stations = delivered_ref.shape
    rows, lanes = last_ref.shape
    basis = gathered_basis(index_ref[0], bands, rows)
    weight = all_ref[:, pl.ds(lanes, 1)]
    destination = all_ref[:, pl.ds(lanes + 1, 1)]
    fit = fit_ref[:, pl.ds(0, rows)]
    terms = fit.shape[0]
    gains = last_ref[...]
    dual = dual_ref[...]
    before = fresh_ref[...]
    coefficients = jnp.dot(
        fit, gains + dual, precision=highest, preferred_element_type=f32
    )
    fresh = jnp.dot(
        basis[:, :terms], coefficients, precision=highest, preferred_element_type=f32
    )
    line = lax.broadcasted_iota(jnp.int32, (rows, lanes), 1)
    start = jnp.where((line // stations) % 2 == 0, 1.0, 0.0)
    pieces = [dual * dual, (before - start) ** 2, (gains - fresh) ** 2, (fresh - before) ** 2]
    lane = lax.broadcasted_iota(jnp.int32, (1, LANES), 1)
    norms = jnp.zeros((1, LANES), f32)
    for n, piece in enumerate(pieces):
        norms = jnp.where(lane == n, jnp.sum(piece * weight), norms)
    norms = jnp.where(lane == len(pieces), jnp.sum(weight), norms)
    norm_ref[...] = norms
    for k in range(dirs):
        for a in range(2):
            part = slice((2 * k + a) * stations, (2 * k + a + 1) * stations)
            for c in range(DEGREE + 1):
                coefficients_ref[c, k, pl.ds(a, 1), :] = coefficients[c : c + 1, part]
    for f in range(bands):
        target = (index_ref[0] * bands + f).astype(f32)
        chosen = jnp.sum(jnp.where(destination == target, gains, 0.0), axis=0, keepdims=True)
        for k in range(dirs):
            for a in range(2):
                part = slice((2 * k + a) * stations, (2 * k + a + 1) * stations)
                delivered_ref[f, k, pl.ds(a, 1), :] = chosen[:, part]


def exchange(x, axis, distance):
    size = lax.axis_size(axis)
    return lax.ppermute(x, axis, [(i ^ distance, i) for i in range(size)])


def gather_rows(x, axis):
    size = lax.axis_size(axis)
    distance = 1
    while distance < size:
        x = jnp.concatenate([x, exchange(x, axis, distance)], axis=0)
        distance *= 2
    return x


def add_over(x, axis):
    size = lax.axis_size(axis)
    distance = 1
    while distance < size:
        x = x + exchange(x, axis, distance)
        distance *= 2
    return x


def vmem(*_):
    return pl.BlockSpec(memory_space=pltpu.VMEM)


def smem():
    return pl.BlockSpec(memory_space=pltpu.SMEM)


def per_device(visibilities, sky_model, rfi_flags, destination):
    bands, dirs, _, stations, _ = visibilities.shape
    count = lax.axis_size("band")
    rows = bands * count
    lanes = dirs * 2 * stations
    index = lax.axis_index("band").reshape(1)
    group = 2
    pairs = bands * dirs
    terms = round_up(DEGREE + 1, SUBLANES)
    block = pl.BlockSpec(
        (bands, group, 2, stations, stations), lambda s: (0, s, 0, 0, 0)
    )
    operator, gains = pl.pallas_call(
        first_kernel,
        grid=(dirs // group,),
        out_shape=(
            jax.ShapeDtypeStruct((pairs, 6 * stations, stations), bf16),
            jax.ShapeDtypeStruct((bands, lanes + LANES), f32),
        ),
        in_specs=[smem(), smem(), block, block],
        out_specs=(vmem(), vmem()),
        scratch_shapes=[
            pltpu.VMEM((bands, stations, stations), bf16),
            pltpu.VMEM((4, stations, stations), bf16),
        ],
        compiler_params=pltpu.CompilerParams(
            dimension_semantics=("arbitrary",), vmem_limit_bytes=36 * 2**20
        ),
        name="first",
    )(rfi_flags, destination, visibilities, sky_model)
    everyone = gather_rows(gains, "band")
    gains, fresh, dual, fit = pl.pallas_call(
        second_kernel,
        out_shape=(
            jax.ShapeDtypeStruct((bands, lanes), f32),
            jax.ShapeDtypeStruct((rows, lanes), f32),
            jax.ShapeDtypeStruct((rows, lanes), f32),
            jax.ShapeDtypeStruct((terms, round_up(rows, LANES)), f32),
        ),
        in_specs=[smem(), smem(), vmem(), vmem()],
        out_specs=(vmem(), vmem(), vmem(), vmem()),
        compiler_params=pltpu.CompilerParams(vmem_limit_bytes=36 * 2**20),
        name="second",
    )(index, rfi_flags, everyone, operator)
    last = gather_rows(gains, "band")
    delivered, coefficients, norms = pl.pallas_call(
        third_kernel,
        out_shape=(
            jax.ShapeDtypeStruct((bands, dirs, 2, stations), f32),
            jax.ShapeDtypeStruct((DEGREE + 1, dirs, 2, stations), f32),
            jax.ShapeDtypeStruct((1, LANES), f32),
        ),
        in_specs=[smem()] + [vmem()] * 5,
        out_specs=(vmem(), vmem(), vmem()),
        compiler_params=pltpu.CompilerParams(vmem_limit_bytes=36 * 2**20),
        name="third",
    )(index, last, everyone, fresh, dual, fit)
    scale = lax.axis_size("dir") * dirs * 2.0 * stations
    totals = add_over(norms, "dir")
    weight_sum = norms[0, 2 * ITERS]
    norm_values = jnp.sqrt(totals[0, : 2 * ITERS] / (scale * weight_sum))
    return delivered, coefficients, norm_values.reshape(ITERS, 2)


def solution(mesh):
    return jax.shard_map(
        per_device,
        mesh=mesh,
        in_specs=(
            P("band", "dir", None, None, None),
            P("band", "dir", None, None, None),
            P("band", None, None),
            P("band"),
        ),
        out_specs=(P("band", "dir", None, None), P(None, "dir", None, None), P()),
        check_vma=False,
    )
```

time: 313 us -> 72.7 us (0.23); the launches traced: 308 us -> 72.3 us
  matrix products: 106 us -> 0 us
  waiting for transfers between devices: 101 us -> 18.7 us
  blocking collectives: 60.4 us -> 0 us
  Pallas kernels: 0 us -> 24.5 us
  between operations: 15.4 us -> 1.35 us
  other arithmetic: 11.9 us -> 0.34 us
  starting transfers between devices: 8.79 us -> 15.9 us
  local copies, waits for them, and re-layouts: 4.65 us -> 11.5 us
    dot_general x22 -> x0, matrix products: 103 us -> none  [the longest x8 58.6 us: stefcal(): jnp.einsum('...kapq,...kbq->...kabp', operator, gain_now, precision=highest)]
    psum x2 -> x0, waiting for transfers between devices: 97 us -> none  [per_device(): projection, gram_matrix = lax.psum((projection, gram_part), 'band')]
    psum x2 -> x0, blocking collectives: 60.4 us -> none  [the longest x1 39.5 us: per_device(): norm_rows.append(lax.psum(local_terms, ('band', 'dir')))]
    pallas_call x0 -> x3, Pallas kernels: none -> 24.5 us  [the longest x1 13.8 us: per_device(): pl.pallas_call(first_kernel, grid=(dirs // group,), out_shape=(jax.ShapeD...]
    ppermute x4 -> x8, waiting for transfers between devices: 3.68 us -> 18.7 us  [exchange(): return lax.ppermute(x, axis, [(i ^ distance, i) for i in range(size)])]
    unnamed x24 -> x12, local copies, waits for them, and re-layouts: 0.09 us -> 10.3 us
    ppermute x4 -> x8, starting transfers between devices: 8.72 us -> 15.9 us  [exchange(): return lax.ppermute(x, axis, [(i ^ distance, i) for i in range(size)])]
    another operation x7 -> x0, other arithmetic: 5.85 us -> none  [the longest x2 2.69 us: per_device(): totals = jnp.stack(norm_rows)]
  transfers between devices with their start and end apart: 6 -> 8, of which waited for: 4 -> 8; matrix products, arithmetic and copies ran while one was open for 25% -> 1% of each run, Pallas kernels for 0% -> 0%
where the time goes in v1:
time: 72.7 us; the launch traced here: 72.3 us
  Pallas kernels  24.5 us (34%)
  waiting for transfers between devices  18.7 us (26%)
  starting transfers between devices  15.9 us (22%)
  local copies, waits for them, and re-layouts  11.5 us (16%)
  between operations  1.35 us (2%)
    ppermute x8, waiting for transfers between devices, exchange(): return lax.ppermute(x, axis, [(i ^ distance, i) for i in range(size)])  18.7 us
    ppermute x8, starting transfers between devices, exchange(): return lax.ppermute(x, axis, [(i ^ distance, i) for i in range(size)])  15.9 us
    pallas_call x1, Pallas kernels, per_device(): pl.pallas_call(first_kernel, grid=(dirs // group,), out_shape=(jax.ShapeD...  13.8 us
    unnamed x12, local copies, waits for them, and re-layouts  10.3 us
    pallas_call x1, Pallas kernels, per_device(): pl.pallas_call(second_kernel, out_shape=(jax.ShapeDtypeStruct((bands, lan...  9.11 us
    pallas_call x1, Pallas kernels, per_device(): pl.pallas_call(third_kernel, out_shape=(jax.ShapeDtypeStruct((bands, dirs...  1.62 us
  transfers between devices with their start and end apart: 8, of which 8 were waited for; matrix products, arithmetic and copies ran while one was open for 1% of the time, Pallas kernels for 0%

profile of v1, /device:TPU:0, one launch (start us, length us, event | category | flops | bytes accessed | tf_op | source)
XLA Modules:
  0.0 72.3 jit_solution(277665899145914917)
XLA Ops:
  0.6 2.2 %copy-done.1 = bf16[2,8,2,256,256]{4,3,2,1,0:T(8,128)(2,1)S(1)} copy-done((bf16[2,8,2,256,256]{4,3,2,1,0:T(8,128)(2,1)S(1)}, bf16[2,8,2,256,256]{4,3,2,1,0:T(8,128)(2,1)}, u32[]{:S(2)}) %copy-start.1) | copy-done | bytes 4194328
  2.8 2.2 %copy-done.2 = bf16[2,8,2,256,256]{4,3,2,1,0:T(8,128)(2,1)S(1)} copy-done((bf16[2,8,2,256,256]{4,3,2,1,0:T(8,128)(2,1)S(1)}, bf16[2,8,2,256,256]{4,3,2,1,0:T(8,128)(2,1)}, u32[]{:S(2)}) %copy-start.2) | copy-done | bytes 4194328
  5.0 0.7 copy-done.3
  5.7 0.7 copy-done.5
  6.4 13.8 %first.1 = (bf16[16,1536,256]{2,1,0:T(8,128)(2,1)}, f32[2,4224]{1,0:T(2,128)S(1)}) custom-call(s32[2,8,8]{2,1,0:T(8,128)S(1)} %copy-done.3, s32[2]{0:T(128)S(1)} %copy-done.5, bf16[2,8,2,256,256]{4,3,2,1,0:T(8,128)(2,1)S(1)} %copy-done.1, bf16[2,8,2,256,256]{4,3,2,1,0:T(8,128)(2,1)S(1)} %copy-done.2), custom_call_target="tpu_custom_call" | custom-call | tf_op jit(solution)/shard_map/first/pallas_call | solution.py:349
  20.2 3.0 %collective-permute-start = (f32[2,4224]{1,0:T(2,128)S(1)}, f32[2,4224]{1,0:T(2,128)S(1)}, u32[]{:S(2)}, u32[]{:S(2)}) collective-permute-start(f32[2,4224]{1,0:T(2,128)S(1)} %get-tuple-element.12), channel_id=1, source_target_pairs={{4,0},{0,4},{12,8},{8,12},{20,16},{16,20},{28,24},{24,28},{5,1},{1... | collective-permute-start | bytes 101384 | tf_op jit(solution)/shard_map/ppermute | solution.py:308
  23.1 1.9 %collective-permute-done = f32[2,4224]{1,0:T(2,128)S(1)} collective-permute-done((f32[2,4224]{1,0:T(2,128)S(1)}, f32[2,4224]{1,0:T(2,128)S(1)}, u32[]{:S(2)}, u32[]{:S(2)}) %collective-permute-start) | collective-permute-done | bytes 33824 | tf_op jit(solution)/shard_map/ppermute | solution.py:308
  25.1 2.2 %collective-permute-start.1 = (f32[4,4224]{1,0:T(4,128)S(1)}, f32[4,4224]{1,0:T(4,128)S(1)}, u32[]{:S(2)}, u32[]{:S(2)}) collective-permute-start(f32[4,4224]{1,0:T(4,128)S(1)} %pad_maximum_fusion.4), channel_id=1, source_target_pairs={{8,0},{12,4},{0,8},{4,12},{24,16},{28,20},{16,24},{20,28},{9,1},{1... | collective-permute-start | bytes 202760 | tf_op jit(solution)/shard_map/ppermute | solution.py:308
  27.3 2.3 %collective-permute-done.1 = f32[4,4224]{1,0:T(4,128)S(1)} collective-permute-done((f32[4,4224]{1,0:T(4,128)S(1)}, f32[4,4224]{1,0:T(4,128)S(1)}, u32[]{:S(2)}, u32[]{:S(2)}) %collective-permute-start.1) | collective-permute-done | bytes 67616 | tf_op jit(solution)/shard_map/ppermute | solution.py:308
  29.6 3.1 %collective-permute-start.2 = (f32[8,4224]{1,0:T(8,128)S(1)}, f32[8,4224]{1,0:T(8,128)S(1)}, u32[]{:S(2)}, u32[]{:S(2)}) collective-permute-start(f32[8,4224]{1,0:T(8,128)S(1)} %pad_maximum_fusion.2), channel_id=1, source_target_pairs={{16,0},{20,4},{24,8},{28,12},{0,16},{4,20},{8,24},{12,28},{17,1},{... | collective-permute-start | bytes 405512 | tf_op jit(solution)/shard_map/ppermute | solution.py:308
  32.7 4.4 %collective-permute-done.2 = f32[8,4224]{1,0:T(8,128)S(1)} collective-permute-done((f32[8,4224]{1,0:T(8,128)S(1)}, f32[8,4224]{1,0:T(8,128)S(1)}, u32[]{:S(2)}, u32[]{:S(2)}) %collective-permute-start.2) | collective-permute-done | bytes 135200 | tf_op jit(solution)/shard_map/ppermute | solution.py:308
  37.2 4.6 %copy-done = bf16[16,1536,256]{2,1,0:T(8,128)(2,1)S(1)} copy-done((bf16[16,1536,256]{2,1,0:T(8,128)(2,1)S(1)}, bf16[16,1536,256]{2,1,0:T(8,128)(2,1)}, u32[]{:S(2)}) %copy-start) | copy-done | bytes 12582936
  41.8 9.1 %second.1 = (f32[2,4096]{1,0:T(2,128)S(1)}, f32[16,4096]{1,0:T(8,128)S(1)}, f32[16,4096]{1,0:T(8,128)S(1)}, f32[16,128]{1,0:T(8,128)S(1)}) custom-call(s32[1]{0:T(128)} %bitcast.index_ref, s32[2,8,8]{2,1,0:T(8,128)S(1)} %copy-done.4, f32[16,4224]{1,0:T(8,128)S(1)} %pad_maximum_fusion.all_ref, bf16[16,1536,256]{2,1,0:T(8,128)(2,1)S(1)} %copy-done), custom_call_target="tpu_custom_call" | custom-call | tf_op jit(solution)/shard_map/second/pallas_call | solution.py:368
  50.9 1.9 %collective-permute-start.3 = (f32[2,4096]{1,0:T(2,128)S(1)}, f32[2,4096]{1,0:T(2,128)S(1)}, u32[]{:S(2)}, u32[]{:S(2)}) collective-permute-start(f32[2,4096]{1,0:T(2,128)S(1)} %get-tuple-element.14), channel_id=1, source_target_pairs={{4,0},{0,4},{12,8},{8,12},{20,16},{16,20},{28,24},{24,28},{5,1},{1... | collective-permute-start | bytes 98312 | tf_op jit(solution)/shard_map/ppermute | solution.py:308
  52.8 2.1 %collective-permute-done.3 = f32[2,4096]{1,0:T(2,128)S(1)} collective-permute-done((f32[2,4096]{1,0:T(2,128)S(1)}, f32[2,4096]{1,0:T(2,128)S(1)}, u32[]{:S(2)}, u32[]{:S(2)}) %collective-permute-start.3) | collective-permute-done | bytes 32800 | tf_op jit(solution)/shard_map/ppermute | solution.py:308
  54.9 1.1 %collective-permute-start.4 = (f32[4,4096]{1,0:T(4,128)S(1)}, f32[4,4096]{1,0:T(4,128)S(1)}, u32[]{:S(2)}, u32[]{:S(2)}) collective-permute-start(f32[4,4096]{1,0:T(4,128)S(1)} %pad_maximum_fusion.5), channel_id=1, source_target_pairs={{8,0},{12,4},{0,8},{4,12},{24,16},{28,20},{16,24},{20,28},{9,1},{1... | collective-permute-start | bytes 196616 | tf_op jit(solution)/shard_map/ppermute | solution.py:308
  56.0 3.3 %collective-permute-done.4 = f32[4,4096]{1,0:T(4,128)S(1)} collective-permute-done((f32[4,4096]{1,0:T(4,128)S(1)}, f32[4,4096]{1,0:T(4,128)S(1)}, u32[]{:S(2)}, u32[]{:S(2)}) %collective-permute-start.4) | collective-permute-done | bytes 65568 | tf_op jit(solution)/shard_map/ppermute | solution.py:308
  59.3 2.9 %collective-permute-start.5 = (f32[8,4096]{1,0:T(8,128)S(1)}, f32[8,4096]{1,0:T(8,128)S(1)}, u32[]{:S(2)}, u32[]{:S(2)}) collective-permute-start(f32[8,4096]{1,0:T(8,128)S(1)} %pad_maximum_fusion.3), channel_id=1, source_target_pairs={{16,0},{20,4},{24,8},{28,12},{0,16},{4,20},{8,24},{12,28},{17,1},{... | collective-permute-start | bytes 393224 | tf_op jit(solution)/shard_map/ppermute | solution.py:308
  62.2 3.1 %collective-permute-done.5 = f32[8,4096]{1,0:T(8,128)S(1)} collective-permute-done((f32[8,4096]{1,0:T(8,128)S(1)}, f32[8,4096]{1,0:T(8,128)S(1)}, u32[]{:S(2)}, u32[]{:S(2)}) %collective-permute-start.5) | collective-permute-done | bytes 131104 | tf_op jit(solution)/shard_map/ppermute | solution.py:308
  65.3 1.6 %third.1 = (f32[2,8,2,256]{3,2,1,0:T(2,128)}, f32[9,8,2,256]{3,2,1,0:T(2,128)}, f32[1,128]{1,0:T(1,128)S(1)}) custom-call(s32[1]{0:T(128)} %bitcast.index_ref, f32[16,4096]{1,0:T(8,128)S(1)} %pad_maximum_fusion.1.last_ref, f32[16,4224]{1,0:T(8,128)S(1)} %pad_maximum_fusion.all_ref, f32[16,4096]{1,0:T(8,128)S(1)} %get-tuple-element.15.fresh_ref, ...), custom_call_target="tpu_custom_call" | custom-call | tf_op jit(solution)/shard_map/third/pallas_call | solution.py:382
  66.9 1.2 %collective-permute-done.6 = f32[1,128]{1,0:T(1,128)S(1)} collective-permute-done((f32[1,128]{1,0:T(1,128)S(1)}, f32[1,128]{1,0:T(1,128)S(1)}, u32[]{:S(2)}, u32[]{:S(2)}) %collective-permute-start.6) | collective-permute-done | bytes 544 | tf_op jit(solution)/shard_map/ppermute | solution.py:308
  68.1 1.8 %collective-permute-start.7 = (f32[1,128]{1,0:T(1,128)S(1)}, f32[1,128]{1,0:T(1,128)S(1)}, u32[]{:S(2)}, u32[]{:S(2)}) collective-permute-start(f32[1,128]{1,0:T(1,128)S(1)} %add.6), channel_id=1, source_target_pairs={{2,0},{3,1},{0,2},{1,3},{6,4},{7,5},{4,6},{5,7},{10,8},{11,9},{8,1... | collective-permute-start | bytes 1544 | tf_op jit(solution)/shard_map/ppermute | solution.py:308
  69.9 0.6 slice.7
  71.7 0.7 sqrt.8
  (18 shorter events, 0.8 us)
Async XLA Ops:
  0.6 2.2 %copy-start.1 = (bf16[2,8,2,256,256]{4,3,2,1,0:T(8,128)(2,1)S(1)}, bf16[2,8,2,256,256]{4,3,2,1,0:T(8,128)(2,1)}, u32[]{:S(2)}) copy-start(bf16[2,8,2,256,256]{4,3,2,1,0:T(8,128)(2,1)} %vis_ref.1) | copy-start | bytes 12582916
  2.8 2.2 %copy-start.2 = (bf16[2,8,2,256,256]{4,3,2,1,0:T(8,128)(2,1)S(1)}, bf16[2,8,2,256,256]{4,3,2,1,0:T(8,128)(2,1)}, u32[]{:S(2)}) copy-start(bf16[2,8,2,256,256]{4,3,2,1,0:T(8,128)(2,1)} %sky_ref.1) | copy-start | bytes 12582916
  5.0 0.7 copy-start.3
  5.7 0.7 copy-start.5
  6.4 30.8 %copy-start.4 = (s32[2,8,8]{2,1,0:T(8,128)S(1)}, s32[2,8,8]{2,1,0:T(8,128)}, u32[]{:S(2)}) copy-start(s32[2,8,8]{2,1,0:T(8,128)} %flags_ref.3) | copy-start | bytes 1540
  20.2 4.9 %collective-permute-start = (f32[2,4224]{1,0:T(2,128)S(1)}, f32[2,4224]{1,0:T(2,128)S(1)}, u32[]{:S(2)}, u32[]{:S(2)}) collective-permute-start(f32[2,4224]{1,0:T(2,128)S(1)} %get-tuple-element.12), channel_id=1, source_target_pairs={{4,0},{0,4},{12,8},{8,12},{20,16},{16,20},{28,24},{24,28},{5,1},{1... | collective-permute-start | bytes 101384 | tf_op jit(solution)/shard_map/ppermute | solution.py:308
  25.1 4.4 %collective-permute-start.1 = (f32[4,4224]{1,0:T(4,128)S(1)}, f32[4,4224]{1,0:T(4,128)S(1)}, u32[]{:S(2)}, u32[]{:S(2)}) collective-permute-start(f32[4,4224]{1,0:T(4,128)S(1)} %pad_maximum_fusion.4), channel_id=1, source_target_pairs={{8,0},{12,4},{0,8},{4,12},{24,16},{28,20},{16,24},{20,28},{9,1},{1... | collective-permute-start | bytes 202760 | tf_op jit(solution)/shard_map/ppermute | solution.py:308
  29.6 7.5 %collective-permute-start.2 = (f32[8,4224]{1,0:T(8,128)S(1)}, f32[8,4224]{1,0:T(8,128)S(1)}, u32[]{:S(2)}, u32[]{:S(2)}) collective-permute-start(f32[8,4224]{1,0:T(8,128)S(1)} %pad_maximum_fusion.2), channel_id=1, source_target_pairs={{16,0},{20,4},{24,8},{28,12},{0,16},{4,20},{8,24},{12,28},{17,1},{... | collective-permute-start | bytes 405512 | tf_op jit(solution)/shard_map/ppermute | solution.py:308
  37.2 4.6 %copy-start = (bf16[16,1536,256]{2,1,0:T(8,128)(2,1)S(1)}, bf16[16,1536,256]{2,1,0:T(8,128)(2,1)}, u32[]{:S(2)}) copy-start(bf16[16,1536,256]{2,1,0:T(8,128)(2,1)} %get-tuple-element.13.oper_ref) | copy-start | bytes 37748740
  50.9 4.0 %collective-permute-start.3 = (f32[2,4096]{1,0:T(2,128)S(1)}, f32[2,4096]{1,0:T(2,128)S(1)}, u32[]{:S(2)}, u32[]{:S(2)}) collective-permute-start(f32[2,4096]{1,0:T(2,128)S(1)} %get-tuple-element.14), channel_id=1, source_target_pairs={{4,0},{0,4},{12,8},{8,12},{20,16},{16,20},{28,24},{24,28},{5,1},{1... | collective-permute-start | bytes 98312 | tf_op jit(solution)/shard_map/ppermute | solution.py:308
  54.9 4.3 %collective-permute-start.4 = (f32[4,4096]{1,0:T(4,128)S(1)}, f32[4,4096]{1,0:T(4,128)S(1)}, u32[]{:S(2)}, u32[]{:S(2)}) collective-permute-start(f32[4,4096]{1,0:T(4,128)S(1)} %pad_maximum_fusion.5), channel_id=1, source_target_pairs={{8,0},{12,4},{0,8},{4,12},{24,16},{28,20},{16,24},{20,28},{9,1},{1... | collective-permute-start | bytes 196616 | tf_op jit(solution)/shard_map/ppermute | solution.py:308
  59.3 5.9 %collective-permute-start.5 = (f32[8,4096]{1,0:T(8,128)S(1)}, f32[8,4096]{1,0:T(8,128)S(1)}, u32[]{:S(2)}, u32[]{:S(2)}) collective-permute-start(f32[8,4096]{1,0:T(8,128)S(1)} %pad_maximum_fusion.3), channel_id=1, source_target_pairs={{16,0},{20,4},{24,8},{28,12},{0,16},{4,20},{8,24},{12,28},{17,1},{... | collective-permute-start | bytes 393224 | tf_op jit(solution)/shard_map/ppermute | solution.py:308
  66.9 1.2 %collective-permute-start.6 = (f32[1,128]{1,0:T(1,128)S(1)}, f32[1,128]{1,0:T(1,128)S(1)}, u32[]{:S(2)}, u32[]{:S(2)}) collective-permute-start(f32[1,128]{1,0:T(1,128)S(1)} %get-tuple-element.20), channel_id=1, source_target_pairs={{1,0},{0,1},{3,2},{2,3},{5,4},{4,5},{7,6},{6,7},{9,8},{8,9},{11,10... | collective-permute-start | bytes 1544 | tf_op jit(solution)/shard_map/ppermute | solution.py:308
  68.1 3.6 %collective-permute-start.7 = (f32[1,128]{1,0:T(1,128)S(1)}, f32[1,128]{1,0:T(1,128)S(1)}, u32[]{:S(2)}, u32[]{:S(2)}) collective-permute-start(f32[1,128]{1,0:T(1,128)S(1)} %add.6), channel_id=1, source_target_pairs={{2,0},{3,1},{0,2},{1,3},{6,4},{7,5},{4,6},{5,7},{10,8},{11,9},{8,1... | collective-permute-start | bytes 1544 | tf_op jit(solution)/shard_map/ppermute | solution.py:308

commit v2 on v1

v2 whole, which is shorter than its diff:
```python
import functools

import jax
import jax.numpy as jnp
from jax import lax
from jax.experimental import pallas as pl
from jax.experimental.pallas import tpu as pltpu
from jax.sharding import PartitionSpec as P

DEGREE = 8
SWEEPS = 4
ITERS = 2
PENALTY_SHARE = 0.4
LANES = 128
SUBLANES = 8
SPAN = 1
GROUP = 16
CHUNK = 32
PARTS = True
SMALL_LIMIT = 12 * 2**20

highest = lax.Precision.HIGHEST
f32 = jnp.float32
bf16 = jnp.bfloat16


def round_up(value, step):
    return -(-value // step) * step


def roll_rows(x, shift):
    return pltpu.roll(x, shift % x.shape[0], 0)


def row_pattern(stations):
    rows = lax.broadcasted_iota(jnp.int32, (SUBLANES, stations), 0)
    even = rows % 2 == 0
    first = rows % 4 < 2
    return even, first


def split_rows(x, even):
    high = x.astype(bf16).astype(f32)
    return jnp.where(even, high, x - high)


def add_pairs(x, even):
    return x + jnp.where(even, roll_rows(x, -1), roll_rows(x, 1))


def weigh_rows(load_square, magnitude):
    stations = magnitude.shape[1]
    column = magnitude.T[:, 0:1]
    total = jnp.zeros((SUBLANES, stations), f32)
    for r in range(stations // SUBLANES):
        part = slice(r * SUBLANES, (r + 1) * SUBLANES)
        total = total + load_square(r * SUBLANES, SUBLANES) * column[part]
    for shift in (4, 2, 1):
        total = total + roll_rows(total, shift)
    return total


def products(load_oper, load_square, load_parts, gain, even, first):
    stations = gain.shape[1]
    halves = split_rows(gain, even)
    crossed = roll_rows(halves, 2)
    crossed = jnp.where(first, -crossed, crossed).astype(bf16)
    halves = halves.astype(bf16)
    lhs = jnp.concatenate([halves, halves, crossed, crossed], axis=1)
    numerator = jnp.dot(lhs, load_oper(0, 4 * stations), preferred_element_type=f32)
    square = gain * gain
    magnitude = square + roll_rows(square, 2)
    if load_parts is None:
        denominator = weigh_rows(load_square, magnitude)
    else:
        lhs = split_rows(magnitude, even).astype(bf16)
        lhs = jnp.concatenate([lhs, lhs], axis=1)
        denominator = jnp.dot(
            lhs, load_parts(0, 2 * stations), preferred_element_type=f32
        )
        denominator = add_pairs(denominator, even)
    return add_pairs(numerator, even), denominator


def update(sums, gain, target_term, pen, average):
    numerator, denominator = sums
    updated = (numerator + target_term) / (denominator + pen)
    return 0.5 * (updated + gain) if average else updated


def to_rows(real, imag, first):
    return jnp.where(first, real, imag)


def band_weight(flags_ref, f, blocks):
    flagged = jnp.int32(0)
    for i in range(blocks):
        for j in range(blocks):
            flagged = flagged + flags_ref[f, i, j]
    kept = (blocks * blocks - flagged).astype(f32)
    return (1.0 + kept) / (1.0 + blocks * blocks)


def turn_steps(vis_ref, sky_ref, mask_ref, turned_ref):
    stations = mask_ref.shape[-1]
    width = LANES

    def turn_sky(a, c):
        part = pl.ds(c * width, width)
        turned_ref[a, part, :] = (sky_ref[a, :, part] * mask_ref[:, part]).T

    def turn_vis(a, c):
        part = pl.ds(c * width, width)
        turned_ref[2 + a, part, :] = vis_ref[a, :, part].T

    return [
        functools.partial(turn, a, c)
        for c in range(stations // width)
        for turn in (turn_sky, turn_vis)
        for a in range(2)
    ]


def combine_steps(turned_ref, oper_ref, square_ref, parts_ref, pen, first, pair, result):
    stations = turned_ref.shape[-1]
    chunk = CHUNK
    totals = [jnp.zeros((SUBLANES, stations), f32) for _ in range(3)]

    def combine(c):
        part = pl.ds(c * chunk, chunk)
        model_re, model_im, data_re, data_im = [
            turned_ref[a, part, :].astype(f32) for a in range(4)
        ]
        values = (
            model_re * data_re + model_im * data_im,
            model_re * data_im - model_im * data_re,
            model_re * model_re + model_im * model_im,
        )
        for n, value in enumerate(values):
            if n == 2:
                square_ref[pair, part, :] = value
            if n < 2 or PARTS:
                high = value.astype(bf16)
                low = (value - high.astype(f32)).astype(bf16)
                target = oper_ref.at[pair] if n < 2 else parts_ref
                start = (2 * n * stations if n < 2 else 0) + c * chunk
                target[pl.ds(start, chunk), :] = high
                target[pl.ds(start + stations, chunk), :] = low
            for r in range(chunk // SUBLANES):
                totals[n] = totals[n] + value[r * SUBLANES : (r + 1) * SUBLANES]

    def finish():
        sums = [jnp.sum(t, axis=0, keepdims=True) for t in totals]
        scale = sums[2] + pen
        result[pair] = to_rows((sums[0] + pen) / scale, sums[1] / scale, first)

    return [functools.partial(combine, c) for c in range(stations // chunk)] + [finish]


def merged(main, side):
    steps = []
    done = 0
    for n, step in enumerate(main):
        until = len(side) * (n + 1) // len(main)
        steps.append(step)
        steps += side[done:until]
        done = until
    return steps + side[done:]


def load_pair(ref, pair):
    return lambda start, size: ref[pair, pl.ds(start, size), :]


def first_kernel(
    flags_hbm, dest_hbm, vis_ref, sky_ref, oper_ref, square_ref, gain_ref,
    vis_buf, sky_buf, mask_ref, turned_ref, parts_ref, flags_ref, dest_ref, vis_sem, sky_sem, small_sem,
):
    bands, dirs, _, stations, _ = vis_ref.shape
    blocks = flags_ref.shape[-1]
    block = stations // blocks
    lanes = gain_ref.shape[1] - LANES
    even, first = row_pattern(stations)
    copies = []
    for k in range(dirs):
        copies.append(
            [
                pltpu.make_async_copy(source.at[:, k], buf.at[:, k], sem.at[k])
                for source, buf, sem in (
                    (sky_ref, sky_buf, sky_sem),
                    (vis_ref, vis_buf, vis_sem),
                )
            ]
        )
    ahead = 4
    for k in range(min(ahead, dirs)):
        for copy in copies[k]:
            copy.start()
    small = [
        pltpu.make_async_copy(flags_hbm, flags_ref, small_sem.at[0]),
        pltpu.make_async_copy(dest_hbm, dest_ref, small_sem.at[1]),
    ]
    for copy in small:
        copy.start()
    for copy in small:
        copy.wait()
    cols = lax.broadcasted_iota(jnp.int32, (block, stations), 1)
    rows = lax.broadcasted_iota(jnp.int32, (block, stations), 0)
    lane = lax.broadcasted_iota(jnp.int32, (1, LANES), 1)
    penalties = []
    for f in range(bands):
        for i in range(blocks):
            keep = jnp.zeros((block, stations), f32)
            for j in range(blocks):
                value = (1 - flags_ref[f, i, j]).astype(f32)
                keep = jnp.where(cols // block == j, value, keep)
            keep = jnp.where(cols == rows + i * block, 0.0, keep)
            mask_ref[f, pl.ds(i * block, block), :] = keep.astype(bf16)
        weight = band_weight(flags_ref, f, blocks)
        penalties.append(PENALTY_SHARE * stations * weight)
        extra = jnp.where(lane == 0, weight, dest_ref[f].astype(f32))
        extra = jnp.where(lane == 2, (lax.axis_index("band") * bands + f).astype(f32), extra)
        gain_ref[pl.ds(f, 1), pl.ds(lanes, LANES)] = extra
    gains = {}

    def sweep_step(pair, index):
        pen = penalties[pair % bands]
        sums = products(
            load_pair(oper_ref, pair),
            load_pair(square_ref, pair),
            load_pair(parts_ref, pair % parts_ref.shape[0]) if PARTS else None,
            gains[pair], even, first,
        )
        gains[pair] = update(
            sums, gains[pair], jnp.where(first, pen, 0.0), pen, index % 2 == 1
        )

    def slot(pair):
        return turned_ref.at[pair % turned_ref.shape[0]]

    def arrive(k):
        for copy in copies[k]:
            copy.wait()
        if k + ahead < dirs:
            for copy in copies[k + ahead]:
                copy.start()

    def turning(pair):
        k, f = divmod(pair, bands)
        steps = turn_steps(vis_buf.at[f, k], sky_buf.at[f, k], mask_ref.at[f], slot(pair))
        return [functools.partial(arrive, k)] * (f == 0) + steps

    def build_set(members):
        steps = [] if members[0] else turning(0)
        for pair in [k * bands + f for k in members for f in range(bands)]:
            combine = combine_steps(
                slot(pair), oper_ref, square_ref, parts_ref.at[pair % parts_ref.shape[0]],
                penalties[pair % bands], first, pair, gains
            )
            steps += merged(combine, turning(pair + 1) if pair + 1 < bands * dirs else [])
        return steps

    def sweep_set(members):
        pairs = [k * bands + f for k in members for f in range(bands)]
        return [
            functools.partial(sweep_step, p, index)
            for index in range(1, SWEEPS)
            for p in pairs
        ]

    sets = [list(range(k, min(k + SPAN, dirs))) for k in range(0, dirs, SPAN)]
    for n in range(len(sets) + 1):
        side = build_set(sets[n]) if n < len(sets) else []
        main = sweep_set(sets[n - 1]) if n else []
        for step in merged(main, side) if main else side:
            step()
        for k in sets[n - 1] if n else ():
            for f in range(bands):
                for a in range(2):
                    gain_ref[pl.ds(f, 1), pl.ds((k * 2 + a) * stations, stations)] = gains[
                        k * bands + f
                    ][2 * a : 2 * a + 1]


def chebyshev_columns(abscissa, width):
    lane = lax.broadcasted_iota(jnp.int32, (abscissa.shape[0], width), 1)
    terms = [jnp.ones_like(abscissa), abscissa]
    for degree in range(2, DEGREE + 1):
        terms.append(2.0 * abscissa * terms[-1] - terms[-2])
    basis = jnp.zeros((abscissa.shape[0], width), f32)
    for degree in range(DEGREE + 1):
        basis = jnp.where(lane == degree, terms[degree], basis)
    return basis


def fit_matrix(basis, weight):
    rows, width = basis.shape
    terms = round_up(DEGREE + 1, SUBLANES)
    span = round_up(rows, LANES)
    lane = lax.broadcasted_iota(jnp.int32, (rows, span), 1)
    row = lax.broadcasted_iota(jnp.int32, (rows, span), 0)
    identity = jnp.where(lane == row, 1.0, 0.0)
    weighted = basis * weight
    right = jnp.concatenate([basis, identity], axis=1)
    system = lax.dot_general(
        weighted, right, (((0,), (0,)), ((), ())), precision=highest,
        preferred_element_type=f32,
    )[:terms]
    line = lax.broadcasted_iota(jnp.int32, system.shape, 0)
    for j in range(DEGREE + 1):
        pivot = system[j : j + 1] / system[j : j + 1, j : j + 1]
        system = jnp.where(line == j, pivot, system - system[:, j : j + 1] * pivot)
    return system[:, width : width + rows], system[0:1, 0:1]


def assemble(pieces, all_ref):
    start = 0
    for piece in pieces:
        all_ref[pl.ds(start, piece.shape[0]), :] = piece[...]
        start += piece.shape[0]


def second_kernel(
    count, oper_ref, square_ref, *refs
):
    gain_ref, fresh_ref, dual_ref, fit_ref, extra_ref, all_ref = refs[count:]
    assemble(refs[:count], all_ref)
    bands = gain_ref.shape[0]
    lanes = gain_ref.shape[1]
    rows = all_ref.shape[0]
    pairs = oper_ref.shape[0]
    stations = oper_ref.shape[2]
    even, first = row_pattern(stations)
    basis = gathered_basis(all_ref[:, pl.ds(lanes, LANES)])
    weight = all_ref[:, pl.ds(lanes, 1)]
    extra_ref[...] = all_ref[:, pl.ds(lanes, LANES)]
    fit, _ = fit_matrix(basis, weight)
    fit_ref[...] = jnp.zeros_like(fit_ref)
    fit_ref[:, pl.ds(0, rows)] = fit
    project = jnp.dot(
        basis[:, : fit.shape[0]], fit, precision=highest, preferred_element_type=f32
    )
    own = all_ref[:, pl.ds(0, lanes)]
    fresh = jnp.dot(project, own, precision=highest, preferred_element_type=f32)
    fresh_ref[...] = fresh
    dual_ref[...] = own - fresh
    group = min(GROUP, pairs)
    for start in range(0, pairs, group):
        gains = []
        targets = []
        penalties = []
        for pair in range(start, start + group):
            k, f = divmod(pair, bands)
            pen = PENALTY_SHARE * stations * all_ref[pl.ds(f, 1), pl.ds(lanes, 1)]
            parts = [pl.ds((2 * k + a) * stations, stations) for a in range(2)]
            line = pl.ds(f, 1)
            gains.append(
                to_rows(all_ref[line, parts[0]], all_ref[line, parts[1]], first)
            )
            goal = [fresh_ref[line, p] - dual_ref[line, p] for p in parts]
            targets.append(pen * to_rows(goal[0], goal[1], first))
            penalties.append(pen)
        for index in range(SWEEPS):
            for n in range(group):
                sums = products(
                    load_pair(oper_ref, start + n), load_pair(square_ref, start + n), None,
                    gains[n], even, first,
                )
                gains[n] = update(sums, gains[n], targets[n], penalties[n], index % 2 == 1)
        for n in range(group):
            k, f = divmod(start + n, bands)
            for a in range(2):
                gain_ref[pl.ds(f, 1), pl.ds((2 * k + a) * stations, stations)] = gains[n][
                    2 * a : 2 * a + 1
                ]


def gathered_basis(extra):
    abscissa = (2.0 * extra[:, 2:3] + 1.0) / extra.shape[0] - 1.0
    return chebyshev_columns(abscissa, LANES)


def third_kernel(count, extra_ref, fresh_ref, dual_ref, fit_ref, *refs):
    delivered_ref, coefficients_ref, norm_ref, last_ref = refs[count:]
    assemble(refs[:count], last_ref)
    bands, dirs, _, stations = delivered_ref.shape
    rows, lanes = last_ref.shape
    extra = extra_ref[...]
    basis = gathered_basis(extra)
    weight, destination = extra[:, 0:1], extra[:, 1:2]
    fit = fit_ref[:, pl.ds(0, rows)]
    terms = fit.shape[0]
    gains = last_ref[...]
    dual = dual_ref[...]
    before = fresh_ref[...]
    coefficients = jnp.dot(
        fit, gains + dual, precision=highest, preferred_element_type=f32
    )
    fresh = jnp.dot(
        basis[:, :terms], coefficients, precision=highest, preferred_element_type=f32
    )
    line = lax.broadcasted_iota(jnp.int32, (rows, lanes), 1)
    start = jnp.where((line // stations) % 2 == 0, 1.0, 0.0)
    pieces = [dual * dual, (before - start) ** 2, (gains - fresh) ** 2, (fresh - before) ** 2]
    lane = lax.broadcasted_iota(jnp.int32, norm_ref.shape, 1)
    line = lax.broadcasted_iota(jnp.int32, norm_ref.shape, 0)
    norms = jnp.zeros(norm_ref.shape, f32)
    for n, piece in enumerate(pieces):
        here = (line == n // 2) & (lane == n % 2)
        norms = jnp.where(here, jnp.sum(piece * weight), norms)
    size = lax.axis_size("dir") * lanes
    norm_ref[...] = norms / (size * jnp.sum(weight))
    for k in range(dirs):
        for a in range(2):
            part = slice((2 * k + a) * stations, (2 * k + a + 1) * stations)
            for c in range(DEGREE + 1):
                coefficients_ref[c, k, pl.ds(a, 1), :] = coefficients[c : c + 1, part]
    for f in range(bands):
        target = extra[f : f + 1, 2:3]
        chosen = jnp.sum(jnp.where(destination == target, gains, 0.0), axis=0, keepdims=True)
        for k in range(dirs):
            for a in range(2):
                part = slice((2 * k + a) * stations, (2 * k + a + 1) * stations)
                delivered_ref[f, k, pl.ds(a, 1), :] = chosen[:, part]


def exchange(x, axis, distance):
    size = lax.axis_size(axis)
    return lax.ppermute(x, axis, [(i ^ distance, i) for i in range(size)])


def gather_rows(x, axis):
    size = lax.axis_size(axis)
    assert size & (size - 1) == 0
    distances = [2**n for n in range(size.bit_length() - 1)]
    for distance in distances[1:-1]:
        x = jnp.concatenate([x, exchange(x, axis, distance)], axis=0)
    if len(distances) == 1:
        return [x, exchange(x, axis, distances[0])]
    if len(distances) > 1:
        far = exchange(x, axis, distances[-1])
        near = exchange(x, axis, distances[0])
        return [x, near, far, exchange(far, axis, distances[0])]
    return [x]


def add_over(x, axis):
    size = lax.axis_size(axis)
    distance = 1
    while distance < size:
        x = x + exchange(x, axis, distance)
        distance *= 2
    return x


def vmem(*_):
    return pl.BlockSpec(memory_space=pltpu.VMEM)


def in_hbm(x):
    return pltpu.with_memory_space_constraint(x, pltpu.HBM)


def smem():
    return pl.BlockSpec(memory_space=pltpu.SMEM)


def per_device(visibilities, sky_model, rfi_flags, destination):
    bands, dirs, _, stations, _ = visibilities.shape
    count = lax.axis_size("band")
    rows = bands * count
    lanes = dirs * 2 * stations
    pairs = bands * dirs
    terms = round_up(DEGREE + 1, SUBLANES)
    hbm = pl.BlockSpec(memory_space=pltpu.HBM)
    operator, square, gains = pl.pallas_call(
        first_kernel,
        out_shape=(
            pltpu.VMEM((pairs, 4 * stations, stations), bf16),
            pltpu.VMEM((pairs, stations, stations), f32),
            jax.ShapeDtypeStruct((bands, lanes + LANES), f32),
        ),
        in_specs=[hbm, hbm, hbm, hbm],
        out_specs=(vmem(), vmem(), vmem()),
        scratch_shapes=[
            pltpu.VMEM((bands, dirs, 2, stations, stations), bf16),
            pltpu.VMEM((bands, dirs, 2, stations, stations), bf16),
            pltpu.VMEM((bands, stations, stations), bf16),
            pltpu.VMEM((2 * SPAN * bands, 4, stations, stations), bf16),
            pltpu.VMEM((2 * SPAN * bands, 2 * stations, stations), bf16),
            pltpu.SMEM(rfi_flags.shape, jnp.int32),
            pltpu.SMEM(destination.shape, jnp.int32),
            pltpu.SemaphoreType.DMA((dirs,)),
            pltpu.SemaphoreType.DMA((dirs,)),
            pltpu.SemaphoreType.DMA((2,)),
        ],
        compiler_params=pltpu.CompilerParams(vmem_limit_bytes=28 * 2**20),
        name="first",
    )(in_hbm(rfi_flags), in_hbm(destination), in_hbm(visibilities), in_hbm(sky_model))
    operator, square = [
        pltpu.with_memory_space_constraint(x, pltpu.VMEM) for x in (operator, square)
    ]
    pieces = gather_rows(gains, "band")
    gains, fresh, dual, fit, extra = pl.pallas_call(
        functools.partial(second_kernel, len(pieces)),
        out_shape=(
            pltpu.VMEM((bands, lanes), f32),
            pltpu.VMEM((rows, lanes), f32),
            pltpu.VMEM((rows, lanes), f32),
            pltpu.VMEM((terms, round_up(rows, LANES)), f32),
            pltpu.VMEM((rows, LANES), f32),
        ),
        in_specs=[vmem()] * (2 + len(pieces)),
        out_specs=(vmem(),) * 5,
        scratch_shapes=[pltpu.VMEM((rows, lanes + LANES), f32)],
        compiler_params=pltpu.CompilerParams(vmem_limit_bytes=SMALL_LIMIT),
        name="second",
    )(operator, square, *pieces)
    pieces = gather_rows(gains, "band")
    delivered, coefficients, norms = pl.pallas_call(
        functools.partial(third_kernel, len(pieces)),
        out_shape=(
            pltpu.VMEM((bands, dirs, 2, stations), f32),
            pltpu.VMEM((DEGREE + 1, dirs, 2, stations), f32),
            pltpu.VMEM((ITERS, LANES), f32),
        ),
        in_specs=[vmem()] * (4 + len(pieces)),
        out_specs=(vmem(),) * 3,
        scratch_shapes=[pltpu.VMEM((rows, lanes), f32)],
        compiler_params=pltpu.CompilerParams(vmem_limit_bytes=SMALL_LIMIT),
        name="third",
    )(extra, fresh, dual, fit, *pieces)
    norm_values = jnp.sqrt(add_over(norms, "dir")[:, :2])
    return delivered, coefficients, norm_values


def solution(mesh):
    return jax.shard_map(
        per_device,
        mesh=mesh,
        in_specs=(
            P("band", "dir", None, None, None),
            P("band", "dir", None, None, None),
            P("band", None, None),
            P("band"),
        ),
        out_specs=(P("band", "dir", None, None), P(None, "dir", None, None), P()),
        check_vma=False,
    )
```

time: 72.7 us -> 52.2 us (0.72)
  local copies, waits for them, and re-layouts: 11.5 us -> 1.85 us
  Pallas kernels: 24.5 us -> 17.1 us
  waiting for transfers between devices: 18.7 us -> 13.7 us
  starting transfers between devices: 15.9 us -> 18.6 us
    unnamed x12 -> x2, local copies, waits for them, and re-layouts: 10.3 us -> 1.27 us
    pallas_call x3, Pallas kernels: 24.5 us -> 17.1 us  [the longest x1 9.54 us: per_device(): pl.pallas_call(first_kernel, out_shape=(pltpu.VMEM((pairs, 4 * stations,...]
    ppermute x8 -> x10, waiting for transfers between devices: 18.7 us -> 13.7 us  [exchange(): return lax.ppermute(x, axis, [(i ^ distance, i) for i in range(size)])]
    ppermute x8 -> x10, starting transfers between devices: 15.9 us -> 18.6 us  [exchange(): return lax.ppermute(x, axis, [(i ^ distance, i) for i in range(size)])]
  transfers between devices with their start and end apart: 8 -> 10, of which waited for: 8 -> 10; matrix products, arithmetic and copies ran while one was open for 1% -> 2% of each run, Pallas kernels for 0% -> 0%
where the time goes in v2:
time: 52.2 us; the launch traced here: 52 us
  starting transfers between devices  18.6 us (36%)
  Pallas kernels  17.1 us (33%)
  waiting for transfers between devices  13.7 us (26%)
  local copies, waits for them, and re-layouts  1.85 us (4%)
  between operations  0.68 us (1%)
    ppermute x10, starting transfers between devices, exchange(): return lax.ppermute(x, axis, [(i ^ distance, i) for i in range(size)])  18.6 us
    ppermute x10, waiting for transfers between devices, exchange(): return lax.ppermute(x, axis, [(i ^ distance, i) for i in range(size)])  13.7 us
    pallas_call x1, Pallas kernels, per_device(): pl.pallas_call(first_kernel, out_shape=(pltpu.VMEM((pairs, 4 * stations,...  9.54 us
    pallas_call x1, Pallas kernels, per_device(): pl.pallas_call(functools.partial(second_kernel, len(pieces)), out_shape=(...  6.61 us
    unnamed x2, local copies, waits for them, and re-layouts  1.27 us
  transfers between devices with their start and end apart: 10, of which 10 were waited for; matrix products, arithmetic and copies ran while one was open for 2% of the time, Pallas kernels for 0%

profile of v2, /device:TPU:0, one launch (start us, length us, event | category | flops | bytes accessed | tf_op | source)
XLA Modules:
  0.0 52.0 jit_solution(889206142197815852)
XLA Ops:
  0.6 9.5 %first.1 = (bf16[16,1024,256]{2,1,0:T(8,128)(2,1)S(1)}, f32[16,256,256]{2,1,0:T(8,128)S(1)}, f32[2,4224]{1,0:T(2,128)S(1)}) custom-call(s32[2,8,8]{2,1,0:T(8,128)} %flags_hbm.1, s32[2]{0:T(128)} %dest_hbm.1, bf16[2,8,2,256,256]{4,3,2,1,0:T(8,128)(2,1)} %vis_ref.1, bf16[2,8,2,256,256]{4,3,2,1,0:T(8,128)(2,1)} %sky_ref.1), custom_call_target="tpu_custom_call" | custom-call | tf_op jit(solution)/shard_map/first/pallas_call | solution.py:476
  10.2 3.1 %collective-permute-start = (f32[2,4224]{1,0:T(2,128)S(1)}, f32[2,4224]{1,0:T(2,128)S(1)}, u32[]{:S(2)}, u32[]{:S(2)}) collective-permute-start(f32[2,4224]{1,0:T(2,128)S(1)} %get-tuple-element.16), channel_id=1, source_target_pairs={{8,0},{12,4},{0,8},{4,12},{24,16},{28,20},{16,24},{20,28},{9,1},{1... | collective-permute-start | bytes 101384 | tf_op jit(solution)/shard_map/ppermute | solution.py:429
  13.3 1.9 %collective-permute-done = f32[2,4224]{1,0:T(2,128)S(1)} collective-permute-done((f32[2,4224]{1,0:T(2,128)S(1)}, f32[2,4224]{1,0:T(2,128)S(1)}, u32[]{:S(2)}, u32[]{:S(2)}) %collective-permute-start) | collective-permute-done | bytes 33824 | tf_op jit(solution)/shard_map/ppermute | solution.py:429
  15.2 3.1 %collective-permute-start.2 = (f32[4,4224]{1,0:T(4,128)S(1)}, f32[4,4224]{1,0:T(4,128)S(1)}, u32[]{:S(2)}, u32[]{:S(2)}) collective-permute-start(f32[4,4224]{1,0:T(4,128)S(1)} %pad_maximum_fusion.refs_0_), channel_id=1, source_target_pairs={{16,0},{20,4},{24,8},{28,12},{0,16},{4,20},{8,24},{12,28},{17,1},{... | collective-permute-start | bytes 202760 | tf_op jit(solution)/shard_map/ppermute | solution.py:429
  18.3 1.5 %collective-permute-start.1 = (f32[4,4224]{1,0:T(4,128)S(1)}, f32[4,4224]{1,0:T(4,128)S(1)}, u32[]{:S(2)}, u32[]{:S(2)}) collective-permute-start(f32[4,4224]{1,0:T(4,128)S(1)} %pad_maximum_fusion.refs_0_), channel_id=1, source_target_pairs={{4,0},{0,4},{12,8},{8,12},{20,16},{16,20},{28,24},{24,28},{5,1},{1... | collective-permute-start | bytes 202760 | tf_op jit(solution)/shard_map/ppermute | solution.py:429
  19.8 0.8 %collective-permute-done.2.refs_2_ = f32[4,4224]{1,0:T(4,128)S(1)} collective-permute-done((f32[4,4224]{1,0:T(4,128)S(1)}, f32[4,4224]{1,0:T(4,128)S(1)}, u32[]{:S(2)}, u32[]{:S(2)}) %collective-permute-start.2) | collective-permute-done | bytes 67616 | tf_op jit(solution)/shard_map/ppermute | solution.py:429
  20.6 1.8 %collective-permute-start.3 = (f32[4,4224]{1,0:T(4,128)S(1)}, f32[4,4224]{1,0:T(4,128)S(1)}, u32[]{:S(2)}, u32[]{:S(2)}) collective-permute-start(f32[4,4224]{1,0:T(4,128)S(1)} %collective-permute-done.2.refs_2_), channel_id=1, source_target_pairs={{4,0},{0,4},{12,8},{8,12},{20,16},{16,20},{28,24},{24,28},{5,1},{1... | collective-permute-start | bytes 202760 | tf_op jit(solution)/shard_map/ppermute | solution.py:429
  22.4 0.2 collective-permute-done.1.refs_1_
  22.6 2.3 %collective-permute-done.3.refs_3_ = f32[4,4224]{1,0:T(4,128)S(1)} collective-permute-done((f32[4,4224]{1,0:T(4,128)S(1)}, f32[4,4224]{1,0:T(4,128)S(1)}, u32[]{:S(2)}, u32[]{:S(2)}) %collective-permute-start.3) | collective-permute-done | bytes 67616 | tf_op jit(solution)/shard_map/ppermute | solution.py:429
  24.9 6.6 %second.1 = (f32[2,4096]{1,0:T(2,128)S(1)}, f32[16,4096]{1,0:T(8,128)S(1)}, f32[16,4096]{1,0:T(8,128)S(1)}, f32[16,128]{1,0:T(8,128)S(1)}, f32[16,128]{1,0:T(8,128)S(1)}) custom-call(bf16[16,1024,256]{2,1,0:T(8,128)(2,1)S(1)} %get-tuple-element.14.oper_ref, f32[16,256,256]{2,1,0:T(8,128)S(1)} %get-tuple-element.15.square_ref, ...), custom_call_target="tpu_custom_call" | custom-call | tf_op jit(solution)/shard_map/second/pallas_call | solution.py:504
  31.5 2.0 %collective-permute-start.4 = (f32[2,4096]{1,0:T(2,128)S(1)}, f32[2,4096]{1,0:T(2,128)S(1)}, u32[]{:S(2)}, u32[]{:S(2)}) collective-permute-start(f32[2,4096]{1,0:T(2,128)S(1)} %get-tuple-element.21), channel_id=1, source_target_pairs={{8,0},{12,4},{0,8},{4,12},{24,16},{28,20},{16,24},{20,28},{9,1},{1... | collective-permute-start | bytes 98312 | tf_op jit(solution)/shard_map/ppermute | solution.py:429
  33.5 2.6 %collective-permute-done.4 = f32[2,4096]{1,0:T(2,128)S(1)} collective-permute-done((f32[2,4096]{1,0:T(2,128)S(1)}, f32[2,4096]{1,0:T(2,128)S(1)}, u32[]{:S(2)}, u32[]{:S(2)}) %collective-permute-start.4) | collective-permute-done | bytes 32800 | tf_op jit(solution)/shard_map/ppermute | solution.py:429
  36.1 2.5 %collective-permute-start.6 = (f32[4,4096]{1,0:T(4,128)S(1)}, f32[4,4096]{1,0:T(4,128)S(1)}, u32[]{:S(2)}, u32[]{:S(2)}) collective-permute-start(f32[4,4096]{1,0:T(4,128)S(1)} %pad_maximum_fusion.1.refs_0_), channel_id=1, source_target_pairs={{16,0},{20,4},{24,8},{28,12},{0,16},{4,20},{8,24},{12,28},{17,1},{... | collective-permute-start | bytes 196616 | tf_op jit(solution)/shard_map/ppermute | solution.py:429
  38.7 1.5 %collective-permute-start.5 = (f32[4,4096]{1,0:T(4,128)S(1)}, f32[4,4096]{1,0:T(4,128)S(1)}, u32[]{:S(2)}, u32[]{:S(2)}) collective-permute-start(f32[4,4096]{1,0:T(4,128)S(1)} %pad_maximum_fusion.1.refs_0_), channel_id=1, source_target_pairs={{4,0},{0,4},{12,8},{8,12},{20,16},{16,20},{28,24},{24,28},{5,1},{1... | collective-permute-start | bytes 196616 | tf_op jit(solution)/shard_map/ppermute | solution.py:429
  40.2 1.2 %collective-permute-done.6.refs_2_ = f32[4,4096]{1,0:T(4,128)S(1)} collective-permute-done((f32[4,4096]{1,0:T(4,128)S(1)}, f32[4,4096]{1,0:T(4,128)S(1)}, u32[]{:S(2)}, u32[]{:S(2)}) %collective-permute-start.6) | collective-permute-done | bytes 65568 | tf_op jit(solution)/shard_map/ppermute | solution.py:429
  41.4 1.5 %collective-permute-start.7 = (f32[4,4096]{1,0:T(4,128)S(1)}, f32[4,4096]{1,0:T(4,128)S(1)}, u32[]{:S(2)}, u32[]{:S(2)}) collective-permute-start(f32[4,4096]{1,0:T(4,128)S(1)} %collective-permute-done.6.refs_2_), channel_id=1, source_target_pairs={{4,0},{0,4},{12,8},{8,12},{20,16},{16,20},{28,24},{24,28},{5,1},{1... | collective-permute-start | bytes 196616 | tf_op jit(solution)/shard_map/ppermute | solution.py:429
  42.9 2.7 %collective-permute-done.7.refs_3_ = f32[4,4096]{1,0:T(4,128)S(1)} collective-permute-done((f32[4,4096]{1,0:T(4,128)S(1)}, f32[4,4096]{1,0:T(4,128)S(1)}, u32[]{:S(2)}, u32[]{:S(2)}) %collective-permute-start.7) | collective-permute-done | bytes 65568 | tf_op jit(solution)/shard_map/ppermute | solution.py:429
  45.6 1.0 %third.1 = (f32[2,8,2,256]{3,2,1,0:T(2,128)S(1)}, f32[9,8,2,256]{3,2,1,0:T(2,128)S(1)}, f32[2,128]{1,0:T(2,128)S(1)}) custom-call(f32[16,128]{1,0:T(8,128)S(1)} %get-tuple-element.17.extra_ref, f32[16,4096]{1,0:T(8,128)S(1)} %get-tuple-element.18.fresh_ref, f32[16,4096]{1,0:T(8,128)S(1)} %get-tuple-element.19.dual_ref, ...), custom_call_target="tpu_custom_call" | custom-call | tf_op jit(solution)/shard_map/third/pallas_call | solution.py:520
  46.7 1.1 %collective-permute-done.8 = f32[2,128]{1,0:T(2,128)S(1)} collective-permute-done((f32[2,128]{1,0:T(2,128)S(1)}, f32[2,128]{1,0:T(2,128)S(1)}, u32[]{:S(2)}, u32[]{:S(2)}) %collective-permute-start.8) | collective-permute-done | bytes 1056 | tf_op jit(solution)/shard_map/ppermute | solution.py:429
  47.9 1.5 %collective-permute-start.9 = (f32[2,128]{1,0:T(2,128)S(1)}, f32[2,128]{1,0:T(2,128)S(1)}, u32[]{:S(2)}, u32[]{:S(2)}) collective-permute-start(f32[2,128]{1,0:T(2,128)S(1)} %add.6), channel_id=1, source_target_pairs={{2,0},{3,1},{0,2},{1,3},{6,4},{7,5},{4,6},{5,7},{10,8},{11,9},{8,1... | collective-permute-start | bytes 3080 | tf_op jit(solution)/shard_map/ppermute | solution.py:429
  49.4 0.6 %copy.7 = f32[2,8,2,256]{3,2,1,0:T(2,128)} copy(f32[2,8,2,256]{3,2,1,0:T(2,128)S(1)} %get-tuple-element.25) | data formatting | bytes 65536
  50.0 0.7 %copy.8 = f32[9,8,2,256]{3,2,1,0:T(2,128)} copy(f32[9,8,2,256]{3,2,1,0:T(2,128)S(1)} %get-tuple-element.26) | data formatting | bytes 294912
  50.7 0.8 %collective-permute-done.9 = f32[2,128]{1,0:T(2,128)S(1)} collective-permute-done((f32[2,128]{1,0:T(2,128)S(1)}, f32[2,128]{1,0:T(2,128)S(1)}, u32[]{:S(2)}, u32[]{:S(2)}) %collective-permute-start.9) | collective-permute-done | bytes 1056 | tf_op jit(solution)/shard_map/ppermute | solution.py:429
  51.5 0.6 %slice_sqrt_fusion = f32[2,2]{1,0:T(2,128)} fusion(f32[2,128]{1,0:T(2,128)S(1)} %add.7), kind=kLoop, calls=%fused_computation.2 | loop fusion | bytes 32 | tf_op jit(solution)/shard_map/sqrt | solution.py:533
  (6 shorter events, 0.2 us)
Async XLA Ops:
  10.2 5.0 %collective-permute-start = (f32[2,4224]{1,0:T(2,128)S(1)}, f32[2,4224]{1,0:T(2,128)S(1)}, u32[]{:S(2)}, u32[]{:S(2)}) collective-permute-start(f32[2,4224]{1,0:T(2,128)S(1)} %get-tuple-element.16), channel_id=1, source_target_pairs={{8,0},{12,4},{0,8},{4,12},{24,16},{28,20},{16,24},{20,28},{9,1},{1... | collective-permute-start | bytes 101384 | tf_op jit(solution)/shard_map/ppermute | solution.py:429
  15.2 5.4 %collective-permute-start.2 = (f32[4,4224]{1,0:T(4,128)S(1)}, f32[4,4224]{1,0:T(4,128)S(1)}, u32[]{:S(2)}, u32[]{:S(2)}) collective-permute-start(f32[4,4224]{1,0:T(4,128)S(1)} %pad_maximum_fusion.refs_0_), channel_id=1, source_target_pairs={{16,0},{20,4},{24,8},{28,12},{0,16},{4,20},{8,24},{12,28},{17,1},{... | collective-permute-start | bytes 202760 | tf_op jit(solution)/shard_map/ppermute | solution.py:429
  18.3 4.3 %collective-permute-start.1 = (f32[4,4224]{1,0:T(4,128)S(1)}, f32[4,4224]{1,0:T(4,128)S(1)}, u32[]{:S(2)}, u32[]{:S(2)}) collective-permute-start(f32[4,4224]{1,0:T(4,128)S(1)} %pad_maximum_fusion.refs_0_), channel_id=1, source_target_pairs={{4,0},{0,4},{12,8},{8,12},{20,16},{16,20},{28,24},{24,28},{5,1},{1... | collective-permute-start | bytes 202760 | tf_op jit(solution)/shard_map/ppermute | solution.py:429
  20.6 4.3 %collective-permute-start.3 = (f32[4,4224]{1,0:T(4,128)S(1)}, f32[4,4224]{1,0:T(4,128)S(1)}, u32[]{:S(2)}, u32[]{:S(2)}) collective-permute-start(f32[4,4224]{1,0:T(4,128)S(1)} %collective-permute-done.2.refs_2_), channel_id=1, source_target_pairs={{4,0},{0,4},{12,8},{8,12},{20,16},{16,20},{28,24},{24,28},{5,1},{1... | collective-permute-start | bytes 202760 | tf_op jit(solution)/shard_map/ppermute | solution.py:429
  31.5 4.6 %collective-permute-start.4 = (f32[2,4096]{1,0:T(2,128)S(1)}, f32[2,4096]{1,0:T(2,128)S(1)}, u32[]{:S(2)}, u32[]{:S(2)}) collective-permute-start(f32[2,4096]{1,0:T(2,128)S(1)} %get-tuple-element.21), channel_id=1, source_target_pairs={{8,0},{12,4},{0,8},{4,12},{24,16},{28,20},{16,24},{20,28},{9,1},{1... | collective-permute-start | bytes 98312 | tf_op jit(solution)/shard_map/ppermute | solution.py:429
  36.1 5.2 %collective-permute-start.6 = (f32[4,4096]{1,0:T(4,128)S(1)}, f32[4,4096]{1,0:T(4,128)S(1)}, u32[]{:S(2)}, u32[]{:S(2)}) collective-permute-start(f32[4,4096]{1,0:T(4,128)S(1)} %pad_maximum_fusion.1.refs_0_), channel_id=1, source_target_pairs={{16,0},{20,4},{24,8},{28,12},{0,16},{4,20},{8,24},{12,28},{17,1},{... | collective-permute-start | bytes 196616 | tf_op jit(solution)/shard_map/ppermute | solution.py:429
  38.7 4.3 %collective-permute-start.5 = (f32[4,4096]{1,0:T(4,128)S(1)}, f32[4,4096]{1,0:T(4,128)S(1)}, u32[]{:S(2)}, u32[]{:S(2)}) collective-permute-start(f32[4,4096]{1,0:T(4,128)S(1)} %pad_maximum_fusion.1.refs_0_), channel_id=1, source_target_pairs={{4,0},{0,4},{12,8},{8,12},{20,16},{16,20},{28,24},{24,28},{5,1},{1... | collective-permute-start | bytes 196616 | tf_op jit(solution)/shard_map/ppermute | solution.py:429
  41.4 4.3 %collective-permute-start.7 = (f32[4,4096]{1,0:T(4,128)S(1)}, f32[4,4096]{1,0:T(4,128)S(1)}, u32[]{:S(2)}, u32[]{:S(2)}) collective-permute-start(f32[4,4096]{1,0:T(4,128)S(1)} %collective-permute-done.6.refs_2_), channel_id=1, source_target_pairs={{4,0},{0,4},{12,8},{8,12},{20,16},{16,20},{28,24},{24,28},{5,1},{1... | collective-permute-start | bytes 196616 | tf_op jit(solution)/shard_map/ppermute | solution.py:429
  46.6 1.2 %collective-permute-start.8 = (f32[2,128]{1,0:T(2,128)S(1)}, f32[2,128]{1,0:T(2,128)S(1)}, u32[]{:S(2)}, u32[]{:S(2)}) collective-permute-start(f32[2,128]{1,0:T(2,128)S(1)} %get-tuple-element.24), channel_id=1, source_target_pairs={{1,0},{0,1},{3,2},{2,3},{5,4},{4,5},{7,6},{6,7},{9,8},{8,9},{11,10... | collective-permute-start | bytes 3080 | tf_op jit(solution)/shard_map/ppermute | solution.py:429
  47.9 3.6 %collective-permute-start.9 = (f32[2,128]{1,0:T(2,128)S(1)}, f32[2,128]{1,0:T(2,128)S(1)}, u32[]{:S(2)}, u32[]{:S(2)}) collective-permute-start(f32[2,128]{1,0:T(2,128)S(1)} %add.6), channel_id=1, source_target_pairs={{2,0},{3,1},{0,2},{1,3},{6,4},{7,5},{4,6},{5,7},{10,8},{11,9},{8,1... | collective-permute-start | bytes 3080 | tf_op jit(solution)/shard_map/ppermute | solution.py:429

commit v3 on v2

--- a/solution.py
+++ b/solution.py
@@ -17,6 +17,7 @@
 GROUP = 16
 CHUNK = 32
 PARTS = True
+AHEAD_FLOPS = 2 * 10**8
 SMALL_LIMIT = 12 * 2**20
 
 highest = lax.Precision.HIGHEST
@@ -192,16 +193,16 @@
                 )
             ]
         )
-    ahead = 4
-    for k in range(min(ahead, dirs)):
-        for copy in copies[k]:
-            copy.start()
     small = [
         pltpu.make_async_copy(flags_hbm, flags_ref, small_sem.at[0]),
         pltpu.make_async_copy(dest_hbm, dest_ref, small_sem.at[1]),
     ]
     for copy in small:
         copy.start()
+    ahead = 2
+    for k in range(min(ahead, dirs)):
+        for copy in copies[k]:
+            copy.start()
     for copy in small:
         copy.wait()
     cols = lax.broadcasted_iota(jnp.int32, (block, stations), 1)
@@ -282,6 +283,25 @@
                     ][2 * a : 2 * a + 1]
 
 
+def load_gain(gain_ref, pair, bands, stations, first):
+    k, f = divmod(pair, bands)
+    real, imag = [
+        gain_ref[pl.ds(f, 1), pl.ds((2 * k + a) * stations, stations)] for a in range(2)
+    ]
+    return to_rows(real, imag, first)
+
+
+def ahead_kernel(oper_ref, square_ref, gain_ref, numerator_ref, denominator_ref):
+    bands = gain_ref.shape[0]
+    pairs, stations, _ = square_ref.shape
+    even, first = row_pattern(stations)
+    for pair in range(pairs):
+        numerator_ref[pair], denominator_ref[pair] = products(
+            load_pair(oper_ref, pair), load_pair(square_ref, pair), None,
+            load_gain(gain_ref, pair, bands, stations, first), even, first,
+        )
+
+
 def chebyshev_columns(abscissa, width):
     lane = lax.broadcasted_iota(jnp.int32, (abscissa.shape[0], width), 1)
     terms = [jnp.ones_like(abscissa), abscissa]
@@ -320,9 +340,7 @@
         start += piece.shape[0]
 
 
-def second_kernel(
-    count, oper_ref, square_ref, *refs
-):
+def second_kernel(count, oper_ref, square_ref, numerator_ref, denominator_ref, *refs):
     gain_ref, fresh_ref, dual_ref, fit_ref, extra_ref, all_ref = refs[count:]
     assemble(refs[:count], all_ref)
     bands = gain_ref.shape[0]
@@ -354,18 +372,19 @@
             pen = PENALTY_SHARE * stations * all_ref[pl.ds(f, 1), pl.ds(lanes, 1)]
             parts = [pl.ds((2 * k + a) * stations, stations) for a in range(2)]
             line = pl.ds(f, 1)
-            gains.append(
-                to_rows(all_ref[line, parts[0]], all_ref[line, parts[1]], first)
-            )
+            gains.append(load_gain(all_ref, pair, bands, stations, first))
             goal = [fresh_ref[line, p] - dual_ref[line, p] for p in parts]
             targets.append(pen * to_rows(goal[0], goal[1], first))
             penalties.append(pen)
         for index in range(SWEEPS):
             for n in range(group):
-                sums = products(
-                    load_pair(oper_ref, start + n), load_pair(square_ref, start + n), None,
-                    gains[n], even, first,
-                )
+                if index == 0:
+                    sums = numerator_ref[start + n], denominator_ref[start + n]
+                else:
+                    sums = products(
+                        load_pair(oper_ref, start + n), load_pair(square_ref, start + n), None,
+                        gains[n], even, first,
+                    )
                 gains[n] = update(sums, gains[n], targets[n], penalties[n], index % 2 == 1)
         for n in range(group):
             k, f = divmod(start + n, bands)
@@ -501,6 +520,17 @@
         pltpu.with_memory_space_constraint(x, pltpu.VMEM) for x in (operator, square)
     ]
     pieces = gather_rows(gains, "band")
+    sums = pl.pallas_call(
+        ahead_kernel,
+        out_shape=(pltpu.VMEM((pairs, SUBLANES, stations), f32),) * 2,
+        in_specs=[vmem()] * 3,
+        out_specs=(vmem(),) * 2,
+        compiler_params=pltpu.CompilerParams(vmem_limit_bytes=SMALL_LIMIT),
+        cost_estimate=pl.CostEstimate(
+            flops=AHEAD_FLOPS, bytes_accessed=0, transcendentals=0
+        ),
+        name="ahead",
+    )(operator, square, gains)
     gains, fresh, dual, fit, extra = pl.pallas_call(
         functools.partial(second_kernel, len(pieces)),
         out_shape=(
@@ -510,12 +540,12 @@
             pltpu.VMEM((terms, round_up(rows, LANES)), f32),
             pltpu.VMEM((rows, LANES), f32),
         ),
-        in_specs=[vmem()] * (2 + len(pieces)),
+        in_specs=[vmem()] * (4 + len(pieces)),
         out_specs=(vmem(),) * 5,
         scratch_shapes=[pltpu.VMEM((rows, lanes + LANES), f32)],
         compiler_params=pltpu.CompilerParams(vmem_limit_bytes=SMALL_LIMIT),
         name="second",
-    )(operator, square, *pieces)
+    )(operator, square, *sums, *pieces)
     pieces = gather_rows(gains, "band")
     delivered, coefficients, norms = pl.pallas_call(
         functools.partial(third_kernel, len(pieces)),

time: 52.2 us -> 51.4 us (0.985)
  waiting for transfers between devices: 13.7 us -> 12.4 us
    ppermute x10, waiting for transfers between devices: 13.7 us -> 12.4 us  [exchange(): return lax.ppermute(x, axis, [(i ^ distance, i) for i in range(size)])]
    pallas_call x0 -> x1, Pallas kernels: none -> 1.24 us  [per_device(): pl.pallas_call(ahead_kernel, out_shape=(pltpu.VMEM((pairs, SUBLANES, stat...]
    pallas_call x1, Pallas kernels: 6.61 us -> 5.77 us  [per_device(): pl.pallas_call(functools.partial(second_kernel, len(pieces)), out_shape=(...]
  transfers between devices with their start and end apart: 10 -> 10, of which waited for: 10 -> 9; matrix products, arithmetic and copies ran while one was open for 2% -> 2% of each run, Pallas kernels for 0% -> 2%
where the time goes in v3:
time: 51.4 us; the launch traced here: 51.2 us
  starting transfers between devices  18.6 us (36%)
  Pallas kernels  17.6 us (34%)
  waiting for transfers between devices  12.4 us (24%)
  local copies, waits for them, and re-layouts  1.85 us (4%)
  between operations  0.68 us (1%)
    ppermute x10, starting transfers between devices, exchange(): return lax.ppermute(x, axis, [(i ^ distance, i) for i in range(size)])  18.6 us
    ppermute x10, waiting for transfers between devices, exchange(): return lax.ppermute(x, axis, [(i ^ distance, i) for i in range(size)])  12.4 us
    pallas_call x1, Pallas kernels, per_device(): pl.pallas_call(first_kernel, out_shape=(pltpu.VMEM((pairs, 4 * stations,...  9.54 us
    pallas_call x1, Pallas kernels, per_device(): pl.pallas_call(functools.partial(second_kernel, len(pieces)), out_shape=(...  5.77 us
    unnamed x2, local copies, waits for them, and re-layouts  1.27 us
    pallas_call x1, Pallas kernels, per_device(): pl.pallas_call(ahead_kernel, out_shape=(pltpu.VMEM((pairs, SUBLANES, stat...  1.24 us
  transfers between devices with their start and end apart: 10, of which 9 were waited for; matrix products, arithmetic and copies ran while one was open for 2% of the time, Pallas kernels for 2%

profile of v3, /device:TPU:0, one launch (start us, length us, event | category | flops | bytes accessed | tf_op | source)
XLA Modules:
  0.0 51.2 jit_solution(576641526913784217)
XLA Ops:
  0.6 9.5 %first.1 = (bf16[16,1024,256]{2,1,0:T(8,128)(2,1)S(1)}, f32[16,256,256]{2,1,0:T(8,128)S(1)}, f32[2,4224]{1,0:T(2,128)S(1)}) custom-call(s32[2,8,8]{2,1,0:T(8,128)} %flags_hbm.1, s32[2]{0:T(128)} %dest_hbm.1, bf16[2,8,2,256,256]{4,3,2,1,0:T(8,128)(2,1)} %vis_ref.1, bf16[2,8,2,256,256]{4,3,2,1,0:T(8,128)(2,1)} %sky_ref.1), custom_call_target="tpu_custom_call" | custom-call | tf_op jit(solution)/shard_map/first/pallas_call | solution.py:495
  10.2 3.1 %collective-permute-start = (f32[2,4224]{1,0:T(2,128)S(1)}, f32[2,4224]{1,0:T(2,128)S(1)}, u32[]{:S(2)}, u32[]{:S(2)}) collective-permute-start(f32[2,4224]{1,0:T(2,128)S(1)} %get-tuple-element.18.gain_ref), channel_id=1, source_target_pairs={{8,0},{12,4},{0,8},{4,12},{24,16},{28,20},{16,24},{20,28},{9,1},{1... | collective-permute-start | bytes 101384 | tf_op jit(solution)/shard_map/ppermute | solution.py:448
  13.3 1.9 %collective-permute-done = f32[2,4224]{1,0:T(2,128)S(1)} collective-permute-done((f32[2,4224]{1,0:T(2,128)S(1)}, f32[2,4224]{1,0:T(2,128)S(1)}, u32[]{:S(2)}, u32[]{:S(2)}) %collective-permute-start) | collective-permute-done | bytes 33824 | tf_op jit(solution)/shard_map/ppermute | solution.py:448
  15.2 3.1 %collective-permute-start.2 = (f32[4,4224]{1,0:T(4,128)S(1)}, f32[4,4224]{1,0:T(4,128)S(1)}, u32[]{:S(2)}, u32[]{:S(2)}) collective-permute-start(f32[4,4224]{1,0:T(4,128)S(1)} %pad_maximum_fusion.refs_0_), channel_id=1, source_target_pairs={{16,0},{20,4},{24,8},{28,12},{0,16},{4,20},{8,24},{12,28},{17,1},{... | collective-permute-start | bytes 202760 | tf_op jit(solution)/shard_map/ppermute | solution.py:448
  18.3 1.5 %collective-permute-start.1 = (f32[4,4224]{1,0:T(4,128)S(1)}, f32[4,4224]{1,0:T(4,128)S(1)}, u32[]{:S(2)}, u32[]{:S(2)}) collective-permute-start(f32[4,4224]{1,0:T(4,128)S(1)} %pad_maximum_fusion.refs_0_), channel_id=1, source_target_pairs={{4,0},{0,4},{12,8},{8,12},{20,16},{16,20},{28,24},{24,28},{5,1},{1... | collective-permute-start | bytes 202760 | tf_op jit(solution)/shard_map/ppermute | solution.py:448
  19.8 0.8 %collective-permute-done.2.refs_2_ = f32[4,4224]{1,0:T(4,128)S(1)} collective-permute-done((f32[4,4224]{1,0:T(4,128)S(1)}, f32[4,4224]{1,0:T(4,128)S(1)}, u32[]{:S(2)}, u32[]{:S(2)}) %collective-permute-start.2) | collective-permute-done | bytes 67616 | tf_op jit(solution)/shard_map/ppermute | solution.py:448
  20.6 1.8 %collective-permute-start.3 = (f32[4,4224]{1,0:T(4,128)S(1)}, f32[4,4224]{1,0:T(4,128)S(1)}, u32[]{:S(2)}, u32[]{:S(2)}) collective-permute-start(f32[4,4224]{1,0:T(4,128)S(1)} %collective-permute-done.2.refs_2_), channel_id=1, source_target_pairs={{4,0},{0,4},{12,8},{8,12},{20,16},{16,20},{28,24},{24,28},{5,1},{1... | collective-permute-start | bytes 202760 | tf_op jit(solution)/shard_map/ppermute | solution.py:448
  22.4 1.2 %ahead.1 = (f32[16,8,256]{2,1,0:T(8,128)S(1)}, f32[16,8,256]{2,1,0:T(8,128)S(1)}) custom-call(bf16[16,1024,256]{2,1,0:T(8,128)(2,1)S(1)} %get-tuple-element.16.oper_ref, f32[16,256,256]{2,1,0:T(8,128)S(1)} %get-tuple-element.17.square_ref, f32[2,4224]{1,0:T(2,128)S(1)} %get-tuple-element.18.gain_ref), custom_call_target="tpu_custom_call" | custom-call | flops 200000000 | tf_op jit(solution)/shard_map/ahead/pallas_call | solution.py:523
  23.7 1.2 %collective-permute-done.3.refs_3_ = f32[4,4224]{1,0:T(4,128)S(1)} collective-permute-done((f32[4,4224]{1,0:T(4,128)S(1)}, f32[4,4224]{1,0:T(4,128)S(1)}, u32[]{:S(2)}, u32[]{:S(2)}) %collective-permute-start.3) | collective-permute-done | bytes 67616 | tf_op jit(solution)/shard_map/ppermute | solution.py:448
  24.9 5.8 %second.1 = (f32[2,4096]{1,0:T(2,128)S(1)}, f32[16,4096]{1,0:T(8,128)S(1)}, f32[16,4096]{1,0:T(8,128)S(1)}, f32[16,128]{1,0:T(8,128)S(1)}, f32[16,128]{1,0:T(8,128)S(1)}) custom-call(bf16[16,1024,256]{2,1,0:T(8,128)(2,1)S(1)} %get-tuple-element.16.oper_ref, f32[16,256,256]{2,1,0:T(8,128)S(1)} %get-tuple-element.17.square_ref, ...), custom_call_target="tpu_custom_call" | custom-call | tf_op jit(solution)/shard_map/second/pallas_call | solution.py:534
  30.7 2.0 %collective-permute-start.4 = (f32[2,4096]{1,0:T(2,128)S(1)}, f32[2,4096]{1,0:T(2,128)S(1)}, u32[]{:S(2)}, u32[]{:S(2)}) collective-permute-start(f32[2,4096]{1,0:T(2,128)S(1)} %get-tuple-element.25), channel_id=1, source_target_pairs={{8,0},{12,4},{0,8},{4,12},{24,16},{28,20},{16,24},{20,28},{9,1},{1... | collective-permute-start | bytes 98312 | tf_op jit(solution)/shard_map/ppermute | solution.py:448
  32.6 2.6 %collective-permute-done.4 = f32[2,4096]{1,0:T(2,128)S(1)} collective-permute-done((f32[2,4096]{1,0:T(2,128)S(1)}, f32[2,4096]{1,0:T(2,128)S(1)}, u32[]{:S(2)}, u32[]{:S(2)}) %collective-permute-start.4) | collective-permute-done | bytes 32800 | tf_op jit(solution)/shard_map/ppermute | solution.py:448
  35.3 2.5 %collective-permute-start.6 = (f32[4,4096]{1,0:T(4,128)S(1)}, f32[4,4096]{1,0:T(4,128)S(1)}, u32[]{:S(2)}, u32[]{:S(2)}) collective-permute-start(f32[4,4096]{1,0:T(4,128)S(1)} %pad_maximum_fusion.1.refs_0_), channel_id=1, source_target_pairs={{16,0},{20,4},{24,8},{28,12},{0,16},{4,20},{8,24},{12,28},{17,1},{... | collective-permute-start | bytes 196616 | tf_op jit(solution)/shard_map/ppermute | solution.py:448
  37.8 1.5 %collective-permute-start.5 = (f32[4,4096]{1,0:T(4,128)S(1)}, f32[4,4096]{1,0:T(4,128)S(1)}, u32[]{:S(2)}, u32[]{:S(2)}) collective-permute-start(f32[4,4096]{1,0:T(4,128)S(1)} %pad_maximum_fusion.1.refs_0_), channel_id=1, source_target_pairs={{4,0},{0,4},{12,8},{8,12},{20,16},{16,20},{28,24},{24,28},{5,1},{1... | collective-permute-start | bytes 196616 | tf_op jit(solution)/shard_map/ppermute | solution.py:448
  39.3 1.2 %collective-permute-done.6.refs_2_ = f32[4,4096]{1,0:T(4,128)S(1)} collective-permute-done((f32[4,4096]{1,0:T(4,128)S(1)}, f32[4,4096]{1,0:T(4,128)S(1)}, u32[]{:S(2)}, u32[]{:S(2)}) %collective-permute-start.6) | collective-permute-done | bytes 65568 | tf_op jit(solution)/shard_map/ppermute | solution.py:448
  40.5 1.5 %collective-permute-start.7 = (f32[4,4096]{1,0:T(4,128)S(1)}, f32[4,4096]{1,0:T(4,128)S(1)}, u32[]{:S(2)}, u32[]{:S(2)}) collective-permute-start(f32[4,4096]{1,0:T(4,128)S(1)} %collective-permute-done.6.refs_2_), channel_id=1, source_target_pairs={{4,0},{0,4},{12,8},{8,12},{20,16},{16,20},{28,24},{24,28},{5,1},{1... | collective-permute-start | bytes 196616 | tf_op jit(solution)/shard_map/ppermute | solution.py:448
  42.1 2.7 %collective-permute-done.7.refs_3_ = f32[4,4096]{1,0:T(4,128)S(1)} collective-permute-done((f32[4,4096]{1,0:T(4,128)S(1)}, f32[4,4096]{1,0:T(4,128)S(1)}, u32[]{:S(2)}, u32[]{:S(2)}) %collective-permute-start.7) | collective-permute-done | bytes 65568 | tf_op jit(solution)/shard_map/ppermute | solution.py:448
  44.8 1.0 %third.1 = (f32[2,8,2,256]{3,2,1,0:T(2,128)S(1)}, f32[9,8,2,256]{3,2,1,0:T(2,128)S(1)}, f32[2,128]{1,0:T(2,128)S(1)}) custom-call(f32[16,128]{1,0:T(8,128)S(1)} %get-tuple-element.21.extra_ref, f32[16,4096]{1,0:T(8,128)S(1)} %get-tuple-element.22.fresh_ref, f32[16,4096]{1,0:T(8,128)S(1)} %get-tuple-element.23.dual_ref, ...), custom_call_target="tpu_custom_call" | custom-call | tf_op jit(solution)/shard_map/third/pallas_call | solution.py:550
  45.9 1.1 %collective-permute-done.8 = f32[2,128]{1,0:T(2,128)S(1)} collective-permute-done((f32[2,128]{1,0:T(2,128)S(1)}, f32[2,128]{1,0:T(2,128)S(1)}, u32[]{:S(2)}, u32[]{:S(2)}) %collective-permute-start.8) | collective-permute-done | bytes 1056 | tf_op jit(solution)/shard_map/ppermute | solution.py:448
  47.0 1.5 %collective-permute-start.9 = (f32[2,128]{1,0:T(2,128)S(1)}, f32[2,128]{1,0:T(2,128)S(1)}, u32[]{:S(2)}, u32[]{:S(2)}) collective-permute-start(f32[2,128]{1,0:T(2,128)S(1)} %add.6), channel_id=1, source_target_pairs={{2,0},{3,1},{0,2},{1,3},{6,4},{7,5},{4,6},{5,7},{10,8},{11,9},{8,1... | collective-permute-start | bytes 3080 | tf_op jit(solution)/shard_map/ppermute | solution.py:448
  48.6 0.6 %copy.7 = f32[2,8,2,256]{3,2,1,0:T(2,128)} copy(f32[2,8,2,256]{3,2,1,0:T(2,128)S(1)} %get-tuple-element.29) | data formatting | bytes 65536
  49.2 0.7 %copy.8 = f32[9,8,2,256]{3,2,1,0:T(2,128)} copy(f32[9,8,2,256]{3,2,1,0:T(2,128)S(1)} %get-tuple-element.30) | data formatting | bytes 294912
  49.8 0.8 %collective-permute-done.9 = f32[2,128]{1,0:T(2,128)S(1)} collective-permute-done((f32[2,128]{1,0:T(2,128)S(1)}, f32[2,128]{1,0:T(2,128)S(1)}, u32[]{:S(2)}, u32[]{:S(2)}) %collective-permute-start.9) | collective-permute-done | bytes 1056 | tf_op jit(solution)/shard_map/ppermute | solution.py:448
  50.6 0.6 %slice_sqrt_fusion = f32[2,2]{1,0:T(2,128)} fusion(f32[2,128]{1,0:T(2,128)S(1)} %add.7), kind=kLoop, calls=%fused_computation.2 | loop fusion | bytes 32 | tf_op jit(solution)/shard_map/sqrt | solution.py:563
  (7 shorter events, 0.2 us)
Async XLA Ops:
  10.2 5.0 %collective-permute-start = (f32[2,4224]{1,0:T(2,128)S(1)}, f32[2,4224]{1,0:T(2,128)S(1)}, u32[]{:S(2)}, u32[]{:S(2)}) collective-permute-start(f32[2,4224]{1,0:T(2,128)S(1)} %get-tuple-element.18.gain_ref), channel_id=1, source_target_pairs={{8,0},{12,4},{0,8},{4,12},{24,16},{28,20},{16,24},{20,28},{9,1},{1... | collective-permute-start | bytes 101384 | tf_op jit(solution)/shard_map/ppermute | solution.py:448
  15.2 5.4 %collective-permute-start.2 = (f32[4,4224]{1,0:T(4,128)S(1)}, f32[4,4224]{1,0:T(4,128)S(1)}, u32[]{:S(2)}, u32[]{:S(2)}) collective-permute-start(f32[4,4224]{1,0:T(4,128)S(1)} %pad_maximum_fusion.refs_0_), channel_id=1, source_target_pairs={{16,0},{20,4},{24,8},{28,12},{0,16},{4,20},{8,24},{12,28},{17,1},{... | collective-permute-start | bytes 202760 | tf_op jit(solution)/shard_map/ppermute | solution.py:448
  18.3 5.3 %collective-permute-start.1 = (f32[4,4224]{1,0:T(4,128)S(1)}, f32[4,4224]{1,0:T(4,128)S(1)}, u32[]{:S(2)}, u32[]{:S(2)}) collective-permute-start(f32[4,4224]{1,0:T(4,128)S(1)} %pad_maximum_fusion.refs_0_), channel_id=1, source_target_pairs={{4,0},{0,4},{12,8},{8,12},{20,16},{16,20},{28,24},{24,28},{5,1},{1... | collective-permute-start | bytes 202760 | tf_op jit(solution)/shard_map/ppermute | solution.py:448
  20.6 4.3 %collective-permute-start.3 = (f32[4,4224]{1,0:T(4,128)S(1)}, f32[4,4224]{1,0:T(4,128)S(1)}, u32[]{:S(2)}, u32[]{:S(2)}) collective-permute-start(f32[4,4224]{1,0:T(4,128)S(1)} %collective-permute-done.2.refs_2_), channel_id=1, source_target_pairs={{4,0},{0,4},{12,8},{8,12},{20,16},{16,20},{28,24},{24,28},{5,1},{1... | collective-permute-start | bytes 202760 | tf_op jit(solution)/shard_map/ppermute | solution.py:448
  30.7 4.6 %collective-permute-start.4 = (f32[2,4096]{1,0:T(2,128)S(1)}, f32[2,4096]{1,0:T(2,128)S(1)}, u32[]{:S(2)}, u32[]{:S(2)}) collective-permute-start(f32[2,4096]{1,0:T(2,128)S(1)} %get-tuple-element.25), channel_id=1, source_target_pairs={{8,0},{12,4},{0,8},{4,12},{24,16},{28,20},{16,24},{20,28},{9,1},{1... | collective-permute-start | bytes 98312 | tf_op jit(solution)/shard_map/ppermute | solution.py:448
  35.3 5.2 %collective-permute-start.6 = (f32[4,4096]{1,0:T(4,128)S(1)}, f32[4,4096]{1,0:T(4,128)S(1)}, u32[]{:S(2)}, u32[]{:S(2)}) collective-permute-start(f32[4,4096]{1,0:T(4,128)S(1)} %pad_maximum_fusion.1.refs_0_), channel_id=1, source_target_pairs={{16,0},{20,4},{24,8},{28,12},{0,16},{4,20},{8,24},{12,28},{17,1},{... | collective-permute-start | bytes 196616 | tf_op jit(solution)/shard_map/ppermute | solution.py:448
  37.8 4.3 %collective-permute-start.5 = (f32[4,4096]{1,0:T(4,128)S(1)}, f32[4,4096]{1,0:T(4,128)S(1)}, u32[]{:S(2)}, u32[]{:S(2)}) collective-permute-start(f32[4,4096]{1,0:T(4,128)S(1)} %pad_maximum_fusion.1.refs_0_), channel_id=1, source_target_pairs={{4,0},{0,4},{12,8},{8,12},{20,16},{16,20},{28,24},{24,28},{5,1},{1... | collective-permute-start | bytes 196616 | tf_op jit(solution)/shard_map/ppermute | solution.py:448
  40.5 4.3 %collective-permute-start.7 = (f32[4,4096]{1,0:T(4,128)S(1)}, f32[4,4096]{1,0:T(4,128)S(1)}, u32[]{:S(2)}, u32[]{:S(2)}) collective-permute-start(f32[4,4096]{1,0:T(4,128)S(1)} %collective-permute-done.6.refs_2_), channel_id=1, source_target_pairs={{4,0},{0,4},{12,8},{8,12},{20,16},{16,20},{28,24},{24,28},{5,1},{1... | collective-permute-start | bytes 196616 | tf_op jit(solution)/shard_map/ppermute | solution.py:448
  45.8 1.2 %collective-permute-start.8 = (f32[2,128]{1,0:T(2,128)S(1)}, f32[2,128]{1,0:T(2,128)S(1)}, u32[]{:S(2)}, u32[]{:S(2)}) collective-permute-start(f32[2,128]{1,0:T(2,128)S(1)} %get-tuple-element.28), channel_id=1, source_target_pairs={{1,0},{0,1},{3,2},{2,3},{5,4},{4,5},{7,6},{6,7},{9,8},{8,9},{11,10... | collective-permute-start | bytes 3080 | tf_op jit(solution)/shard_map/ppermute | solution.py:448
  47.0 3.6 %collective-permute-start.9 = (f32[2,128]{1,0:T(2,128)S(1)}, f32[2,128]{1,0:T(2,128)S(1)}, u32[]{:S(2)}, u32[]{:S(2)}) collective-permute-start(f32[2,128]{1,0:T(2,128)S(1)} %add.6), channel_id=1, source_target_pairs={{2,0},{3,1},{0,2},{1,3},{6,4},{7,5},{4,6},{5,7},{10,8},{11,9},{8,1... | collective-permute-start | bytes 3080 | tf_op jit(solution)/shard_map/ppermute | solution.py:448
